TPU v7x, 128 devices: a whole 4x4x4 slice. The times are simulated.
128 devices in a mesh: prow: 8 (over y, core), pcol: 16 (over z, x).
Axes of the slice: x: 4, y: 4, z: 4, core: 2. Of those that a mesh axis runs over, the one named last changes fastest.
Arguments:
- inverse_cov: bfloat16 [8192, 8192], P('prow', 'pcol'), may hold values from -0.5 to 4.5, as said below
- cosines: float32 [8192, 8192], P('prow', 'pcol'), may hold values from -1 to 1, as said below
- sky_maps: bfloat16 [8192, 192], P('pcol'), may hold values from -6 to 6
Outputs:
- filtered: bfloat16 [8192, 192], P('prow')
- spectra: float32 [64, 192], replicated
Inputs may be any that keep to these rules, and one draw needn't show every extreme that they name: `inverse_cov`: symmetric, with a dominant diagonal. `cosines`: symmetric.
All inputs are finite; a program needn't handle non-finite values.
Results may differ from a plain program's by a relative error of at most 0.0033.
Values may be sent and summed in bfloat16 or wider, within the bound.
A program may use at most 64 MiB of HBM per device.

v0:
```python
import functools
import math
import random

import jax
import jax.numpy as jnp
import numpy as np
from jax import lax
from jax.experimental import pallas as pl
from jax.experimental.pallas import tpu as pltpu
from jax.sharding import PartitionSpec as P

L = 64
LMIN = 2
TILE = 256
STRIP = 16
GROUP = 11
CHUNKS = 6
LEVELS = GROUP * CHUNKS


def transform_matrix(npix, devices):
    top = LMIN + L - 1
    each = -(-L // devices)
    a = [math.comb(2 * k, k) / 4.0**k for k in range(top + 1)]
    out = np.zeros((devices * each, LEVELS))
    for l in range(LMIN, top + 1):
        owner, place = divmod(l - LMIN, each)
        row = out[owner * each + place]
        for k in range(l + 1):
            row[abs(l - 2 * k)] += a[k] * a[l - k]
        row *= (2 * l + 1) / npix
    return out.astype(np.float32), each


def pair_up(tiles, n):
    items = []
    for col in range(n):
        mine = sorted((t for t in tiles if t[1] == col), key=lambda t: t[0])
        for k in range(0, len(mine), 2):
            first = mine[k]
            second = mine[k + 1] if k + 1 < len(mine) else (first[0], col, 0)
            items.append((first[0], second[0], first[2], second[2], col))
    return items


def work_tables(n):
    lower = [[(h * n + i, j, 2) for i in range(n) for j in range(n)] for h in range(2)]
    rng = random.Random(0)
    best = None
    for _ in range(20000):
        sets = []
        cross = [[rng.random() < 0.5 for _ in range(n)] for _ in range(n)]
        for h in range(2):
            tiles = []
            for i in range(n):
                tiles.append((h * n + i, i, 1))
                for j in range(i):
                    a, b = (i, j) if rng.random() < 0.5 else (j, i)
                    tiles.append((h * n + a, b, 2))
                for j in range(n):
                    if h == 0 and cross[i][j]:
                        tiles.append((n + i, j, 2))
                    if h == 1 and not cross[i][j]:
                        tiles.append((j, i, 2))
            sets.append(pair_up(tiles, n))
        cost = max(len(s) for s in sets)
        if best is None or cost < best[0]:
            best = (cost, sets)
        if 2 * cost <= n * n + n // 2 + 1:
            break
    kinds = [pair_up(lower[0], n), pair_up(lower[1], n), pair_up(lower[1], n), pair_up(lower[0], n)] + best[1]
    longest = max(len(k) for k in kinds)
    table = np.zeros((len(kinds), longest + 1, 5), np.int32)
    for k, items in enumerate(kinds):
        table[k, : len(items)] = items
    counts = np.array([len(k) for k in kinds], np.int32)
    return table.reshape(-1), counts, longest + 1


def moments_kernel(
    stride, table, counts, cos_hbm, ft, fct, out,
    xbuf, x2, prev, cur, buf_a, buf_b, lhs, fj, acc, sem,
):
    r = lax.axis_index("prow")
    c = lax.axis_index("pcol")
    q, h = c // 2, c % 2
    kind = jnp.where(r > q, h, jnp.where(r < q, 2 + h, 4 + h))
    n_items = counts[kind]

    def field(item, f):
        return table[(kind * stride + item) * 5 + f]

    def tile_copy(item, half):
        row = pl.multiple_of(field(item, half) * TILE, TILE)
        col = pl.multiple_of(field(item, 4) * TILE, TILE)
        return pltpu.make_async_copy(
            cos_hbm.at[pl.ds(row, TILE), pl.ds(col, TILE)],
            xbuf.at[pl.ds(half * TILE, TILE)],
            sem.at[half],
        )

    def fetch(item):
        tile_copy(item, 0).start()
        tile_copy(item, 1).start()

    def begin(item):
        tile_copy(item, 0).wait()
        tile_copy(item, 1).wait()
        x = xbuf[...]
        x2[...] = x + x
        prev[...] = (x + x) * x - 1.0
        cur[...] = x

    def set_operands(item):
        col = pl.multiple_of(field(item, 4) * TILE, TILE)
        for half in range(2):
            row = pl.multiple_of(field(item, half) * TILE, TILE)
            weight = field(item, 2 + half).astype(jnp.float32)
            value = ft[:, pl.ds(row, TILE)].astype(jnp.float32) * weight
            lhs[:, half * TILE : (half + 1) * TILE] = value.astype(jnp.bfloat16)
        fj[...] = fct[:, pl.ds(col, TILE)].astype(jnp.float32)

    n_strips = 2 * TILE // STRIP

    def gen_strip(buf, s):
        rows = pl.ds(s * STRIP, STRIP)
        xx = x2[rows, :]
        p = prev[rows, :]
        t = cur[rows, :]
        for g in range(GROUP):
            p, t = t, xx * t - p
            buf[g, rows, :] = t.astype(jnp.bfloat16)
        prev[rows, :] = p
        cur[rows, :] = t

    def half_step(gen, use, level0):
        done = 0
        for g in range(GROUP):
            upto = (g + 1) * n_strips // GROUP
            for s in range(done, upto):
                gen_strip(gen, s)
            done = upto
            image = jnp.dot(lhs[...], use[g], preferred_element_type=jnp.float32)
            prod = image * fj[...]
            half_tile = TILE // 2
            acc[level0 + g] += prod[:, :half_tile] + prod[:, half_tile:]

    acc[...] = jnp.zeros_like(acc)
    fetch(0)
    begin(0)
    for s in range(n_strips):
        gen_strip(buf_a, s)

    def item_loop(item, carry):
        fetch(item + 1)
        set_operands(item)

        def chunk_loop(cp, carry):
            half_step(buf_b, buf_a, cp * 2 * GROUP)

            @pl.when(cp == CHUNKS // 2 - 1)
            def _():
                begin(item + 1)

            half_step(buf_a, buf_b, cp * 2 * GROUP + GROUP)
            return carry

        return lax.fori_loop(0, CHUNKS // 2, chunk_loop, carry)

    lax.fori_loop(0, n_items, item_loop, 0)
    out[...] = jnp.sum(acc[...], axis=-1)


def spectra_moments(cosines, ft, fct):
    maps = ft.shape[0]
    n = cosines.shape[1] // TILE
    table, counts, stride = work_tables(n)
    vmem = pl.BlockSpec(memory_space=pltpu.VMEM)
    smem = pl.BlockSpec(memory_space=pltpu.SMEM)
    return pl.pallas_call(
        functools.partial(moments_kernel, stride),
        out_shape=jax.ShapeDtypeStruct((LEVELS, maps), jnp.float32),
        in_specs=[smem, smem, pl.BlockSpec(memory_space=pl.ANY), vmem, vmem],
        out_specs=vmem,
        scratch_shapes=[
            pltpu.VMEM((2 * TILE, TILE), jnp.float32),
            pltpu.VMEM((2 * TILE, TILE), jnp.float32),
            pltpu.VMEM((2 * TILE, TILE), jnp.float32),
            pltpu.VMEM((2 * TILE, TILE), jnp.float32),
            pltpu.VMEM((GROUP, 2 * TILE, TILE), jnp.bfloat16),
            pltpu.VMEM((GROUP, 2 * TILE, TILE), jnp.bfloat16),
            pltpu.VMEM((maps, 2 * TILE), jnp.bfloat16),
            pltpu.VMEM((maps, TILE), jnp.float32),
            pltpu.VMEM((LEVELS, maps, TILE // 2), jnp.float32),
            pltpu.SemaphoreType.DMA((2,)),
        ],
        compiler_params=pltpu.CompilerParams(vmem_limit_bytes=48 * 2**20),
        name="moments",
    )(jnp.asarray(table), jnp.asarray(counts), cosines, ft, fct)


MESH = pl.DeviceIdType.MESH


def spread_kernel(n_q, block, out, far_send, near_send, far_recv, side_send, side_recv):
    r = lax.axis_index("prow")
    c = lax.axis_index("pcol")
    q, h = c // 2, c % 2
    width = block.shape[1]
    pieces = far_recv.shape[0]
    step = width // pieces
    partner = (r, c + 1 - 2 * h)
    above, below = (r, c + 2), (r, c - 2)
    has_above, has_below = q < n_q - 1, q > 0
    barrier = pltpu.get_barrier_semaphore()
    pl.semaphore_signal(barrier, inc=1, device_id=partner, device_id_type=MESH)

    @pl.when(has_above)
    def _():
        pl.semaphore_signal(barrier, inc=1, device_id=above, device_id_type=MESH)

    @pl.when(has_below)
    def _():
        pl.semaphore_signal(barrier, inc=1, device_id=below, device_id_type=MESH)

    pl.semaphore_wait(barrier, 1 + has_above.astype(jnp.int32) + has_below.astype(jnp.int32))

    source = q == r
    up = jnp.logical_and(q >= r, has_above)
    down = jnp.logical_and(q <= r, has_below)

    def columns(half, k):
        return pl.ds(pl.multiple_of(half * width + k * step, 128), step)

    def remote(src, k, send, recv, device):
        return pltpu.make_async_remote_copy(
            src_ref=src,
            dst_ref=out.at[:, columns(h, k)],
            send_sem=send.at[k],
            recv_sem=recv.at[k],
            device_id=device,
            device_id_type=MESH,
        )

    def send_all(src, k):
        @pl.when(up)
        def _():
            remote(src, k, far_send, far_recv, above).start()

        @pl.when(down)
        def _():
            remote(src, k, near_send, far_recv, below).start()

        remote(src, k, side_send, side_recv, partner).start()

    @pl.when(source)
    def _():
        for k in range(pieces):
            send_all(block.at[:, pl.ds(k * step, step)], k)
        out[:, pl.ds(pl.multiple_of(h * width, 128), width)] = block[...]

    @pl.when(jnp.logical_not(source))
    def _():
        for k in range(pieces):
            landed = out.at[:, columns(h, k)]
            remote(landed, k, side_send, far_recv, partner).wait_recv()
            send_all(landed, k)

    for k in range(pieces):
        mine = block.at[:, pl.ds(k * step, step)]

        @pl.when(up)
        def _():
            remote(mine, k, far_send, far_recv, above).wait_send()

        @pl.when(down)
        def _():
            remote(mine, k, near_send, far_recv, below).wait_send()

        remote(mine, k, side_send, side_recv, partner).wait_send()
        pltpu.make_async_remote_copy(
            src_ref=mine,
            dst_ref=out.at[:, columns(1 - h, k)],
            send_sem=side_send.at[k],
            recv_sem=side_recv.at[k],
            device_id=partner,
            device_id_type=MESH,
        ).wait_recv()


def spread(block, n_q, collective_id):
    maps, width = block.shape
    pieces = width // 128
    vmem = pl.BlockSpec(memory_space=pltpu.VMEM)
    sems = pltpu.SemaphoreType.DMA((pieces,))
    return pl.pallas_call(
        functools.partial(spread_kernel, n_q),
        out_shape=jax.ShapeDtypeStruct((maps, 2 * width), block.dtype),
        in_specs=[vmem],
        out_specs=vmem,
        scratch_shapes=[sems] * 5,
        compiler_params=pltpu.CompilerParams(
            collective_id=collective_id, has_side_effects=True
        ),
        name="spread%d" % collective_id,
    )(block)


def sum_kernel(n, place_of, device_of, x, out, landed, result, send1, recv1, send2, recv2):
    me = place_of()
    barrier = pltpu.get_barrier_semaphore()

    def each(body):
        lax.fori_loop(1, n, lambda k, carry: (body(k), carry)[1], 0)

    def member(k):
        return device_of(lax.rem(me + k, n))

    each(lambda k: pl.semaphore_signal(barrier, inc=1, device_id=member(k), device_id_type=MESH))
    pl.semaphore_wait(barrier, n - 1)

    def scatter(k):
        return pltpu.make_async_remote_copy(
            src_ref=x.at[lax.rem(me + k, n)],
            dst_ref=landed.at[k - 1],
            send_sem=send1.at[k - 1],
            recv_sem=recv1.at[k - 1],
            device_id=member(k),
            device_id_type=MESH,
        )

    def gather(k, slot):
        return pltpu.make_async_remote_copy(
            src_ref=result,
            dst_ref=out.at[slot],
            send_sem=send2.at[k - 1],
            recv_sem=recv2.at[k - 1],
            device_id=member(k),
            device_id_type=MESH,
        )

    each(lambda k: scatter(k).start())
    each(lambda k: scatter(k).wait_recv())
    total = lax.fori_loop(0, n - 1, lambda k, t: t + landed[k], x[me]) if n > 8 else sum(
        (landed[k] for k in range(n - 1)), x[me]
    )
    result[...] = total.astype(result.dtype)
    each(lambda k: gather(k, me).start())
    out[me] = result[...]
    each(lambda k: gather(k, lax.rem(me - k + n, n)).wait_recv())
    each(lambda k: scatter(k).wait_send())
    each(lambda k: gather(k, me).wait_send())


def pair_kernel(
    n, place_of, device_of, x, out, from_pair, pair_sum, landed, result,
    send1, recv1, send2, recv2, send3, recv3, send4, recv4,
):
    me = place_of()
    m = n // 2
    side, spot = me % 2, me // 2
    partner = device_of(me + 1 - 2 * side)

    def member(k):
        return device_of(lax.rem(spot + k, m) * 2 + side)

    def copy(src, dst, send, recv, device):
        return pltpu.make_async_remote_copy(
            src_ref=src, dst_ref=dst, send_sem=send, recv_sem=recv,
            device_id=device, device_id_type=MESH,
        )

    def first(k):
        j = lax.rem(spot + k, m)
        return copy(x.at[2 * j + 1 - side], from_pair.at[j], send1.at[k - 1], recv1.at[k - 1], partner)

    def second(k):
        return copy(pair_sum.at[k - 1], landed.at[k - 1], send2.at[k - 1], recv2.at[k - 1], member(k))

    def third(k, slot):
        return copy(result, out.at[slot], send3.at[k - 1], recv3.at[k - 1], member(k))

    def fourth(k, parity):
        slot = lax.rem(spot - k + m, m) * 2 + parity
        src = result if k == 0 else out.at[slot]
        return copy(src, out.at[slot], send4.at[k], recv4.at[k], partner)

    barrier = pltpu.get_barrier_semaphore()
    pl.semaphore_signal(barrier, inc=1, device_id=partner, device_id_type=MESH)
    for k in range(1, m):
        pl.semaphore_signal(barrier, inc=1, device_id=member(k), device_id_type=MESH)
    pl.semaphore_wait(barrier, m)
    for k in range(1, m + 1):
        first(k).start()
    for k in range(1, m):
        j = lax.rem(spot + k, m)
        first(k).wait_recv()
        pair_sum[k - 1] = x[2 * j + side] + from_pair[j]
        second(k).start()
    first(m).wait_recv()
    total = x[me] + from_pair[spot]
    for k in range(1, m):
        second(k).wait_recv()
        total = total + landed[k - 1]
    result[...] = total.astype(result.dtype)
    for k in range(1, m):
        third(k, me).start()
    fourth(0, side).start()
    out[me] = result[...]
    for k in range(1, m):
        third(k, lax.rem(spot - k + m, m) * 2 + side).wait_recv()
        fourth(k, side).start()
    for k in range(m):
        fourth(k, 1 - side).wait_recv()
    for k in range(1, m + 1):
        first(k).wait_send()
    for k in range(1, m):
        second(k).wait_send()
        third(k, me).wait_send()
    for k in range(m):
        fourth(k, side).wait_send()


def pair_sum_and_share(x, dtype, place_of, device_of, collective_id):
    n, rows, cols = x.shape
    m = n // 2
    vmem = pl.BlockSpec(memory_space=pltpu.VMEM)
    whole, rest = pltpu.SemaphoreType.DMA((m,)), pltpu.SemaphoreType.DMA((m - 1,))
    return pl.pallas_call(
        functools.partial(pair_kernel, n, place_of, device_of),
        out_shape=jax.ShapeDtypeStruct(x.shape, dtype),
        in_specs=[vmem],
        out_specs=vmem,
        scratch_shapes=[
            pltpu.VMEM((m, rows, cols), x.dtype),
            pltpu.VMEM((m - 1, rows, cols), x.dtype),
            pltpu.VMEM((m - 1, rows, cols), x.dtype),
            pltpu.VMEM((rows, cols), dtype),
            whole, whole, rest, rest, rest, rest, whole, whole,
        ],
        compiler_params=pltpu.CompilerParams(
            collective_id=collective_id, has_side_effects=True
        ),
        name="sum%d" % collective_id,
    )(x)


def sum_and_share(x, dtype, place_of, device_of, collective_id):
    n, rows, cols = x.shape
    vmem = pl.BlockSpec(memory_space=pltpu.VMEM)
    sems = pltpu.SemaphoreType.DMA((n - 1,))
    return pl.pallas_call(
        functools.partial(sum_kernel, n, place_of, device_of),
        out_shape=jax.ShapeDtypeStruct(x.shape, dtype),
        in_specs=[vmem],
        out_specs=vmem,
        scratch_shapes=[
            pltpu.VMEM((n - 1, rows, cols), x.dtype),
            pltpu.VMEM((rows, cols), dtype),
            sems, sems, sems, sems,
        ],
        compiler_params=pltpu.CompilerParams(
            collective_id=collective_id, has_side_effects=True
        ),
        name="sum%d" % collective_id,
    )(x)


def per_device(npix, n_rows, n_cols, inverse_cov, cosines, sky_maps):
    maps = sky_maps.shape[1]
    cols_here = inverse_cov.shape[1]
    n_q = n_cols // 2
    sky_rows = spread(sky_maps.T, n_q, 1)
    partial_value = jnp.dot(sky_rows, inverse_cov, preferred_element_type=jnp.float32)
    column_maps = pair_sum_and_share(
        partial_value.reshape(n_rows, maps // n_rows, cols_here),
        jnp.bfloat16,
        lambda: lax.axis_index("prow"),
        lambda i: (i, lax.axis_index("pcol")),
        2,
    ).reshape(maps, cols_here)
    row_maps = spread(column_maps, n_q, 3)
    moments = spectra_moments(cosines, row_maps, column_maps)
    devices = n_rows * n_cols
    matrix, each = transform_matrix(npix, devices)
    partial_spectra = jnp.dot(jnp.asarray(matrix), moments, precision=lax.Precision.HIGHEST)
    shared = sum_and_share(
        partial_spectra.reshape(devices, each, maps),
        jnp.float32,
        lambda: lax.axis_index("prow") * n_cols + lax.axis_index("pcol"),
        lambda i: (i // n_cols, lax.rem(i, n_cols)),
        4,
    )
    spectra = shared.reshape(devices * each, maps)[:L]
    return (row_maps.T, spectra)


def solution(mesh):
    in_specs = (P("prow", "pcol"), P("prow", "pcol"), P("pcol", None))
    out_specs = (P("prow", None), P())
    n_rows, n_cols = mesh.shape["prow"], mesh.shape["pcol"]

    def whole(inverse_cov, cosines, sky_maps):
        npix = cosines.shape[0]
        step = jax.shard_map(
            functools.partial(per_device, npix, n_rows, n_cols),
            mesh=mesh, in_specs=in_specs, out_specs=out_specs, check_vma=False,
        )
        return step(inverse_cov, cosines, sky_maps)

    return whole
```

profile of v0, /device:TPU:1, one launch (start us, length us, event | category | flops | bytes accessed | tf_op | source)
XLA Modules:
  0.0 153.3 jit_solution(9719502614025576168)
XLA Ops:
  0.6 0.0 copy-start
  0.6 0.0 copy-start.5
  0.7 0.0 copy-start.6
  0.7 0.0 copy-start.3
  0.7 18.5 %spread1.1 = bf16[192,1024]{1,0:T(8,128)(2,1)} custom-call(bf16[192,512]{1,0:T(8,128)(2,1)} %bitcast.17), custom_call_target="tpu_custom_call" | custom-call | tf_op jit(solution)/shard_map/spread1/pallas_call | solution.py:297
  19.2 0.0 copy-done
  19.2 2.1 %fusion = f32[192,512]{1,0:T(8,128)} fusion(bf16[192,1024]{1,0:T(8,128)(2,1)} %spread1.1, bf16[1024,512]{1,0:T(8,128)(2,1)S(1)} %copy-done), kind=kOutput, calls=%fused_computation.2 | convolution fusion | flops 201326592 | bytes 1835008 | tf_op jit(solution)/shard_map/dot_general | solution.py:475
  21.3 41.6 %sum2.1 = bf16[8,24,512]{2,1,0:T(8,128)(2,1)} custom-call(f32[8,24,512]{2,1,0:T(8,128)} %bitcast.16), custom_call_target="tpu_custom_call" | custom-call | tf_op jit(solution)/shard_map/sum2/pallas_call | solution.py:430
  62.9 16.8 %spread3.1.ft = bf16[192,1024]{1,0:T(8,128)(2,1)} custom-call(bf16[192,512]{1,0:T(8,128)(2,1)} %bitcast.14), custom_call_target="tpu_custom_call" | custom-call | tf_op jit(solution)/shard_map/spread3/pallas_call | solution.py:297
  79.7 0.0 copy-done.5
  79.7 0.0 copy-done.6
  79.7 0.0 copy-done.3
  79.7 0.0 copy-start.1
  79.7 1.0 copy-done.1
  80.7 0.0 copy-start.4
  80.7 0.9 copy-done.4
  81.7 0.0 copy-start.2
  81.7 15.3 %moments.1 = f32[66,192]{1,0:T(8,128)S(1)} custom-call(s32[120]{0:T(128)S(1)} %copy-done.5, s32[6]{0:T(128)S(1)} %copy-done.6, f32[1024,512]{1,0:T(8,128)S(1)} %copy-done.3, bf16[192,1024]{1,0:T(8,128)(2,1)S(1)} %copy-done.1, bf16[192,512]{1,0:T(8,128)(2,1)S(1)} %bitcast.15), custom_call_target="tpu_custom_call" | custom-call | tf_op jit(solution)/shard_map/moments/pallas_call | solution.py:181
  96.9 1.2 convolution_bitcast_fusion
  98.1 0.8 copy.9.x
  98.9 52.1 %sum4.1 = f32[128,1,192]{2,1,0:T(1,128)} custom-call(f32[128,1,192]{2,1,0:T(1,128)} %copy.9.x), custom_call_target="tpu_custom_call" | custom-call | tf_op jit(solution)/shard_map/sum4/pallas_call | solution.py:453
  151.0 0.8 slice.6
  151.9 0.6 copy.12
  152.5 0.0 copy-done.2
  152.5 0.7 copy.14
Async XLA Ops:
  0.6 18.5 %copy-start = (bf16[1024,512]{1,0:T(8,128)(2,1)S(1)}, bf16[1024,512]{1,0:T(8,128)(2,1)}, u32[]{:S(2)}) copy-start(bf16[1024,512]{1,0:T(8,128)(2,1)} %param.6) | copy-start | bytes 3145732
  0.6 79.1 %copy-start.5 = (s32[120]{0:T(128)S(1)}, s32[120]{0:T(128)}, u32[]{:S(2)}) copy-start(s32[120]{0:T(128)} %constant.6.clone.table) | copy-start | bytes 1444
  0.7 79.1 %copy-start.6 = (s32[6]{0:T(128)S(1)}, s32[6]{0:T(128)}, u32[]{:S(2)}) copy-start(s32[6]{0:T(128)} %constant.7.clone.counts) | copy-start | bytes 76
  0.7 79.1 %copy-start.3 = (f32[1024,512]{1,0:T(8,128)S(1)}, f32[1024,512]{1,0:T(8,128)}, u32[]{:S(2)}) copy-start(f32[1024,512]{1,0:T(8,128)} %cos_hbm.1) | copy-start | bytes 6291460
  79.7 1.0 copy-start.1
  80.7 0.9 copy-start.4
  81.7 70.8 %copy-start.2 = (bf16[192,1024]{1,0:T(8,128)(2,1)S(1)}, bf16[192,1024]{1,0:T(8,128)(2,1)}, u32[]{:S(2)}) copy-start(bf16[192,1024]{1,0:T(8,128)(2,1)} %spread3.1.ft) | copy-start | bytes 1179652
where the time goes:
time: 154 us; the launch traced here: 153 us
  Pallas kernels  144 us (94%)
  local copies, waits for them, and re-layouts  4.93 us (3%)
  matrix products  3.3 us (2%)
    pallas_call x1, Pallas kernels, sum_and_share(): pl.pallas_call(functools.partial(sum_kernel, n, place_of, device_of), out...  52.1 us
    pallas_call x1, Pallas kernels, pair_sum_and_share(): pl.pallas_call(functools.partial(pair_kernel, n, place_of, device_of), ou...  41.6 us
    pallas_call x2, Pallas kernels, spread(): pl.pallas_call(functools.partial(spread_kernel, n_q), out_shape=jax.Shape...  35.3 us
    pallas_call x1, Pallas kernels, spectra_moments(): pl.pallas_call(functools.partial(moments_kernel, stride), out_shape=jax.S...  15.3 us
    unnamed x16, local copies, waits for them, and re-layouts  3.33 us

commit v1 on v0

v1 whole, which is shorter than its diff:
```python
import functools
import math
import random

import jax
import jax.numpy as jnp
import numpy as np
from jax import lax
from jax.experimental import pallas as pl
from jax.experimental.pallas import tpu as pltpu
from jax.sharding import PartitionSpec as P

L = 64
LMIN = 2
TILE = 256
STRIP = 16
GROUP = 11
CHUNKS = 6
LEVELS = GROUP * CHUNKS


def transform_matrix(npix, devices):
    top = LMIN + L - 1
    each = -(-L // devices)
    a = [math.comb(2 * k, k) / 4.0**k for k in range(top + 1)]
    out = np.zeros((devices * each, LEVELS))
    for l in range(LMIN, top + 1):
        owner, place = divmod(l - LMIN, each)
        row = out[owner * each + place]
        for k in range(l + 1):
            row[abs(l - 2 * k)] += a[k] * a[l - k]
        row *= (2 * l + 1) / npix
    return out.astype(np.float32), each


def pair_up(tiles, n):
    items = []
    for col in range(n):
        mine = sorted((t for t in tiles if t[1] == col), key=lambda t: t[0])
        for k in range(0, len(mine), 2):
            first = mine[k]
            second = mine[k + 1] if k + 1 < len(mine) else (first[0], col, 0)
            items.append((first[0], second[0], first[2], second[2], col))
    return items


def work_tables(n):
    lower = [[(h * n + i, j, 2) for i in range(n) for j in range(n)] for h in range(2)]
    rng = random.Random(0)
    best = None
    for _ in range(20000):
        sets = []
        cross = [[rng.random() < 0.5 for _ in range(n)] for _ in range(n)]
        for h in range(2):
            tiles = []
            for i in range(n):
                tiles.append((h * n + i, i, 1))
                for j in range(i):
                    a, b = (i, j) if rng.random() < 0.5 else (j, i)
                    tiles.append((h * n + a, b, 2))
                for j in range(n):
                    if h == 0 and cross[i][j]:
                        tiles.append((n + i, j, 2))
                    if h == 1 and not cross[i][j]:
                        tiles.append((j, i, 2))
            sets.append(pair_up(tiles, n))
        cost = max(len(s) for s in sets)
        if best is None or cost < best[0]:
            best = (cost, sets)
        if 2 * cost <= n * n + n // 2 + 1:
            break
    kinds = [pair_up(lower[0], n), pair_up(lower[1], n), pair_up(lower[1], n), pair_up(lower[0], n)] + best[1]
    longest = max(len(k) for k in kinds)
    table = np.zeros((len(kinds), longest + 1, 5), np.int32)
    for k, items in enumerate(kinds):
        table[k, : len(items)] = items
    counts = np.array([len(k) for k in kinds], np.int32)
    return table.reshape(-1), counts, longest + 1


def moments_kernel(
    stride, table, counts, cos_hbm, ft, fct, out,
    xbuf, x2, prev, cur, buf_a, buf_b, lhs, fj, acc, sem,
):
    r = lax.axis_index("prow")
    c = lax.axis_index("pcol")
    q, h = c // 2, c % 2
    kind = jnp.where(r > q, h, jnp.where(r < q, 2 + h, 4 + h))
    n_items = counts[kind]

    def field(item, f):
        return table[(kind * stride + item) * 5 + f]

    def tile_copy(item, half):
        row = pl.multiple_of(field(item, half) * TILE, TILE)
        col = pl.multiple_of(field(item, 4) * TILE, TILE)
        return pltpu.make_async_copy(
            cos_hbm.at[pl.ds(row, TILE), pl.ds(col, TILE)],
            xbuf.at[pl.ds(half * TILE, TILE)],
            sem.at[half],
        )

    def fetch(item):
        tile_copy(item, 0).start()
        tile_copy(item, 1).start()

    def begin(item):
        tile_copy(item, 0).wait()
        tile_copy(item, 1).wait()
        x = xbuf[...]
        x2[...] = x + x
        prev[...] = (x + x) * x - 1.0
        cur[...] = x

    def set_operands(item):
        col = pl.multiple_of(field(item, 4) * TILE, TILE)
        for half in range(2):
            row = pl.multiple_of(field(item, half) * TILE, TILE)
            weight = field(item, 2 + half).astype(jnp.float32)
            value = ft[:, pl.ds(row, TILE)].astype(jnp.float32) * weight
            lhs[:, half * TILE : (half + 1) * TILE] = value.astype(jnp.bfloat16)
        fj[...] = fct[:, pl.ds(col, TILE)].astype(jnp.float32)

    n_strips = 2 * TILE // STRIP

    def gen_strip(buf, s):
        rows = pl.ds(s * STRIP, STRIP)
        xx = x2[rows, :]
        p = prev[rows, :]
        t = cur[rows, :]
        for g in range(GROUP):
            p, t = t, xx * t - p
            buf[g, rows, :] = t.astype(jnp.bfloat16)
        prev[rows, :] = p
        cur[rows, :] = t

    def half_step(gen, use, level0):
        done = 0
        for g in range(GROUP):
            upto = (g + 1) * n_strips // GROUP
            for s in range(done, upto):
                gen_strip(gen, s)
            done = upto
            image = jnp.dot(lhs[...], use[g], preferred_element_type=jnp.float32)
            prod = image * fj[...]
            half_tile = TILE // 2
            acc[level0 + g] += prod[:, :half_tile] + prod[:, half_tile:]

    acc[...] = jnp.zeros_like(acc)
    fetch(0)
    begin(0)
    for s in range(n_strips):
        gen_strip(buf_a, s)

    def item_loop(item, carry):
        fetch(item + 1)
        set_operands(item)

        def chunk_loop(cp, carry):
            half_step(buf_b, buf_a, cp * 2 * GROUP)

            @pl.when(cp == CHUNKS // 2 - 1)
            def _():
                begin(item + 1)

            half_step(buf_a, buf_b, cp * 2 * GROUP + GROUP)
            return carry

        return lax.fori_loop(0, CHUNKS // 2, chunk_loop, carry)

    lax.fori_loop(0, n_items, item_loop, 0)
    out[...] = jnp.sum(acc[...], axis=-1)


def spectra_moments(cosines, ft, fct):
    maps = ft.shape[0]
    n = cosines.shape[1] // TILE
    table, counts, stride = work_tables(n)
    vmem = pl.BlockSpec(memory_space=pltpu.VMEM)
    smem = pl.BlockSpec(memory_space=pltpu.SMEM)
    return pl.pallas_call(
        functools.partial(moments_kernel, stride),
        out_shape=jax.ShapeDtypeStruct((LEVELS, maps), jnp.float32),
        in_specs=[smem, smem, pl.BlockSpec(memory_space=pl.ANY), vmem, vmem],
        out_specs=vmem,
        scratch_shapes=[
            pltpu.VMEM((2 * TILE, TILE), jnp.float32),
            pltpu.VMEM((2 * TILE, TILE), jnp.float32),
            pltpu.VMEM((2 * TILE, TILE), jnp.float32),
            pltpu.VMEM((2 * TILE, TILE), jnp.float32),
            pltpu.VMEM((GROUP, 2 * TILE, TILE), jnp.bfloat16),
            pltpu.VMEM((GROUP, 2 * TILE, TILE), jnp.bfloat16),
            pltpu.VMEM((maps, 2 * TILE), jnp.bfloat16),
            pltpu.VMEM((maps, TILE), jnp.float32),
            pltpu.VMEM((LEVELS, maps, TILE // 2), jnp.float32),
            pltpu.SemaphoreType.DMA((2,)),
        ],
        compiler_params=pltpu.CompilerParams(vmem_limit_bytes=48 * 2**20),
        name="moments",
    )(jnp.asarray(table), jnp.asarray(counts), cosines, ft, fct)


MESH = pl.DeviceIdType.MESH


def rank_order(rows, cols):
    spots = [(dz, dx) for dz in range(rows) for dx in range(cols) if dz or dx]
    reach = lambda d, n: min(d, n - d)
    return sorted(spots, key=lambda s: -(reach(s[0], rows) + reach(s[1], cols)))


def filter_kernel(
    n_rows, n_z, n_x, sky, cov, rows_out, cols_out, part, parcel, landed, mine,
    send1, recv1, send2, recv2, send3, recv3,
):
    r = lax.axis_index("prow")
    c = lax.axis_index("pcol")
    n = n_z * n_x
    z, x = c // n_x, lax.rem(c, n_x)
    half_n = n // 2
    maps = sky.shape[1]
    per, width = parcel.shape[1], parcel.shape[2]
    barrier = pltpu.get_barrier_semaphore()
    order = rank_order(n_z, n_x)
    home = c // 2
    from_other = r != home

    def peer(spot):
        return lax.rem(z + spot[0], n_z) * n_x + lax.rem(x + spot[1], n_x)

    def peer_back(spot):
        return lax.rem(z - spot[0] + n_z, n_z) * n_x + lax.rem(x - spot[1] + n_x, n_x)

    def signal(device):
        pl.semaphore_signal(barrier, inc=1, device_id=device, device_id_type=MESH)

    for spot in order:
        signal((r, peer(spot)))

    @pl.when(from_other)
    def _():
        for j in range(half_n):
            signal((home, lax.rem(c, 2) * half_n + j))

    sky_t = sky[...].astype(jnp.float32).T.astype(jnp.bfloat16)
    wide = 2 * width
    for g in range(cov.shape[0] // wide):
        value = lax.dot_general(
            sky_t, cov[g * wide : (g + 1) * wide, :], (((1,), (1,)), ((), ())),
            preferred_element_type=jnp.float32,
        )
        for a in range(2):
            for b in range(maps // per):
                k = (2 * g + a) * (maps // per) + b
                piece = value[b * per : (b + 1) * per, a * width : (a + 1) * width]
                part[k] = piece
                parcel[k] = piece.astype(jnp.bfloat16)

    pl.semaphore_wait(barrier, len(order) + n_rows - 1)

    def copy(src, dst, send, recv, device):
        return pltpu.make_async_remote_copy(
            src_ref=src, dst_ref=dst, send_sem=send, recv_sem=recv,
            device_id=device, device_id_type=MESH,
        )

    def scatter(s):
        to = peer(order[s])
        return copy(parcel.at[to], landed.at[s], send1.at[s], recv1.at[s], (r, to))

    for s in range(len(order)):
        scatter(s).start()
    total = part[c]
    for s in range(len(order)):
        scatter(s).wait_recv()
        total = total + landed[s].astype(jnp.float32)
    mine[...] = total.astype(jnp.bfloat16)

    def row_place(k):
        return rows_out.at[
            pl.ds(pl.multiple_of(lax.rem(k, 2) * per, per), per),
            pl.ds(pl.multiple_of((k // 2) * width, width), width),
        ]

    def col_place(k):
        return cols_out.at[
            pl.ds(pl.multiple_of(lax.rem(k, 2) * per, per), per),
            pl.ds(pl.multiple_of((lax.rem(k, half_n) // 2) * width, width), width),
        ]

    def gather(s, k):
        return copy(mine, row_place(k), send2.at[s], recv2.at[s], (r, peer(order[s])))

    def column(e):
        return copy(
            mine, col_place(c), send3.at[e - 1], recv3.at[lax.rem(c, half_n)],
            (lax.rem(r + e, n_rows), 2 * r + c // half_n),
        )

    far = [4, 5, 3, 2, 6, 1, 7]
    for s in range(8):
        gather(s, c).start()
    for e in far:
        column(e).start()
    for s in range(8, len(order)):
        gather(s, c).start()
    rows_out[
        pl.ds(pl.multiple_of(lax.rem(c, 2) * per, per), per),
        pl.ds(pl.multiple_of((c // 2) * width, width), width),
    ] = mine[...]

    for s in range(len(order)):
        gather(s, peer_back(order[s])).wait_recv()

    @pl.when(from_other)
    def _():
        for j in range(half_n):
            copy(
                mine, col_place(j), send3.at[0], recv3.at[j],
                (home, lax.rem(c, 2) * half_n + j),
            ).wait_recv()

    @pl.when(jnp.logical_not(from_other))
    def _():
        size = cols_out.shape[1]
        cols_out[...] = rows_out[:, pl.ds(pl.multiple_of(lax.rem(c, 2) * size, size), size)]

    for s in range(len(order)):
        scatter(s).wait_send()
        gather(s, c).wait_send()
    for e in far:
        column(e).wait_send()


def filter_maps(sky, cov, n_rows, n_z, n_x, collective_id):
    n = n_z * n_x
    maps, size = sky.shape[1], cov.shape[0]
    per, width = maps // 2, 2 * size // n
    vmem = pl.BlockSpec(memory_space=pltpu.VMEM)
    plane = pltpu.SemaphoreType.DMA((n - 1,))
    return pl.pallas_call(
        functools.partial(filter_kernel, n_rows, n_z, n_x),
        out_shape=(
            jax.ShapeDtypeStruct((maps, size), jnp.bfloat16),
            jax.ShapeDtypeStruct((maps, cov.shape[1]), jnp.bfloat16),
        ),
        in_specs=[vmem, vmem],
        out_specs=(vmem, vmem),
        scratch_shapes=[
            pltpu.VMEM((n, per, width), jnp.float32),
            pltpu.VMEM((n, per, width), jnp.bfloat16),
            pltpu.VMEM((n - 1, per, width), jnp.bfloat16),
            pltpu.VMEM((per, width), jnp.bfloat16),
            plane, plane, plane, plane,
            pltpu.SemaphoreType.DMA((n_rows - 1,)),
            pltpu.SemaphoreType.DMA((n // 2,)),
        ],
        compiler_params=pltpu.CompilerParams(
            collective_id=collective_id, has_side_effects=True
        ),
        name="filter",
    )(sky, cov)


def total_kernel(
    n_rows, n_z, n_x, x, out, landed, mine, others, result,
    send1, recv1, send2, recv2, send3, recv3,
):
    r = lax.axis_index("prow")
    c = lax.axis_index("pcol")
    z, xx = c // n_x, lax.rem(c, n_x)
    order = rank_order(n_z, n_x)
    per = x.shape[0] // n_rows
    barrier = pltpu.get_barrier_semaphore()
    far = [4, 5, 3, 2, 6, 1, 7]

    def peer(spot):
        return lax.rem(z + spot[0], n_z) * n_x + lax.rem(xx + spot[1], n_x)

    def line(e):
        return lax.rem(r + e, n_rows)

    def signal(device):
        pl.semaphore_signal(barrier, inc=1, device_id=device, device_id_type=MESH)

    for spot in order:
        signal((r, peer(spot)))
    for e in far:
        signal((line(e), c))
    pl.semaphore_wait(barrier, len(order) + len(far))

    def block(k):
        return pl.ds(pl.multiple_of(k * per, per), per)

    def copy(src, dst, send, recv, device):
        return pltpu.make_async_remote_copy(
            src_ref=src, dst_ref=dst, send_sem=send, recv_sem=recv,
            device_id=device, device_id_type=MESH,
        )

    def first(e):
        return copy(x.at[block(line(e))], landed.at[e - 1], send1.at[e - 1], recv1.at[e - 1], (line(e), c))

    def second(s):
        return copy(mine, others.at[c], send2.at[s], recv2.at[s], (r, peer(order[s])))

    def third(e, k):
        return copy(result, out.at[block(k)], send3.at[e - 1], recv3.at[e - 1], (line(e), c))

    for e in far:
        first(e).start()
    total = x[block(r)]
    for e in far:
        first(e).wait_recv()
    for e in range(1, n_rows):
        total = total + landed[e - 1]
    mine[...] = total
    for s in range(len(order)):
        second(s).start()
    others[c] = total
    for s in range(len(order)):
        second(s).wait_recv()
    total = others[0]
    for k in range(1, n_z * n_x):
        total = total + others[k]
    result[...] = total
    for e in far:
        third(e, r).start()
    out[block(r)] = total
    for e in far:
        third(e, lax.rem(r - e + n_rows, n_rows)).wait_recv()
    for e in far:
        first(e).wait_send()
        third(e, r).wait_send()
    for s in range(len(order)):
        second(s).wait_send()


def total_over_all(x, n_rows, n_z, n_x, collective_id):
    n = n_z * n_x
    per, cols = x.shape[0] // n_rows, x.shape[1]
    vmem = pl.BlockSpec(memory_space=pltpu.VMEM)
    plane = pltpu.SemaphoreType.DMA((n - 1,))
    line = pltpu.SemaphoreType.DMA((n_rows - 1,))
    return pl.pallas_call(
        functools.partial(total_kernel, n_rows, n_z, n_x),
        out_shape=jax.ShapeDtypeStruct(x.shape, x.dtype),
        in_specs=[vmem],
        out_specs=vmem,
        scratch_shapes=[
            pltpu.VMEM((n_rows - 1, per, cols), x.dtype),
            pltpu.VMEM((per, cols), x.dtype),
            pltpu.VMEM((n, per, cols), x.dtype),
            pltpu.VMEM((per, cols), x.dtype),
            line, line, plane, plane, line, line,
        ],
        compiler_params=pltpu.CompilerParams(
            collective_id=collective_id, has_side_effects=True
        ),
        name="total",
    )(x)


N_X = 4


def per_device(npix, n_rows, n_cols, inverse_cov, cosines, sky_maps):
    n_z = n_cols // N_X
    row_maps, column_maps = filter_maps(sky_maps, inverse_cov, n_rows, n_z, N_X, 1)
    moments = spectra_moments(cosines, row_maps, column_maps)
    matrix, _ = transform_matrix(npix, 1)
    partial_spectra = jnp.dot(jnp.asarray(matrix), moments, precision=lax.Precision.HIGHEST)
    spectra = total_over_all(partial_spectra, n_rows, n_z, N_X, 2)
    return (row_maps.T, spectra)


def solution(mesh):
    in_specs = (P("prow", "pcol"), P("prow", "pcol"), P("pcol", None))
    out_specs = (P("prow", None), P())
    n_rows, n_cols = mesh.shape["prow"], mesh.shape["pcol"]

    def whole(inverse_cov, cosines, sky_maps):
        npix = cosines.shape[0]
        step = jax.shard_map(
            functools.partial(per_device, npix, n_rows, n_cols),
            mesh=mesh, in_specs=in_specs, out_specs=out_specs, check_vma=False,
        )
        return step(inverse_cov, cosines, sky_maps)

    return whole
```

time: 154 us -> 76.2 us (0.49)
  Pallas kernels: 144 us -> 65.5 us
  local copies, waits for them, and re-layouts: 4.93 us -> 8.81 us
  matrix products: 3.3 us -> 0.83 us
    pallas_call x4 -> x2, Pallas kernels: 129 us -> 50.9 us  [the longest x1 26.7 us: filter_maps(): pl.pallas_call(functools.partial(filter_kernel, n_rows, n_z, n_x), out_sh...]
    unnamed x16 -> x17, local copies, waits for them, and re-layouts: 3.33 us -> 8.81 us
    dot_general x1 -> x0, matrix products: 2.12 us -> none  [per_device(): jnp.dot(sky_rows, inverse_cov, preferred_element_type=jnp.float32)]
where the time goes in v1:
time: 76.2 us; the launch traced here: 75.8 us
  Pallas kernels  65.5 us (86%)
  local copies, waits for them, and re-layouts  8.81 us (12%)
  matrix products  0.83 us (1%)
    pallas_call x1, Pallas kernels, filter_maps(): pl.pallas_call(functools.partial(filter_kernel, n_rows, n_z, n_x), out_sh...  26.7 us
    pallas_call x1, Pallas kernels, total_over_all(): pl.pallas_call(functools.partial(total_kernel, n_rows, n_z, n_x), out_sha...  24.2 us
    pallas_call x1, Pallas kernels, spectra_moments(): pl.pallas_call(functools.partial(moments_kernel, stride), out_shape=jax.S...  14.6 us
    unnamed x17, local copies, waits for them, and re-layouts  8.81 us

profile of v1, /device:TPU:1, one launch (start us, length us, event | category | flops | bytes accessed | tf_op | source)
XLA Modules:
  0.0 75.8 jit_solution(12059030602255609409)
XLA Ops:
  0.6 1.8 %copy.8.sky = bf16[512,192]{1,0:T(8,128)(2,1)} copy(bf16[512,192]{0,1:T(8,128)(2,1)} %param.8) | data formatting | bytes 393216 | tf_op args[2]
  2.4 0.0 copy-start.6
  2.4 26.7 %filter.1 = (bf16[192,1024]{1,0:T(8,128)(2,1)}, bf16[192,512]{1,0:T(8,128)(2,1)}) custom-call(bf16[512,192]{1,0:T(8,128)(2,1)} %copy.8.sky, bf16[1024,512]{1,0:T(8,128)(2,1)} %cov.1), custom_call_target="tpu_custom_call" | custom-call | tf_op jit(solution)/shard_map/filter/pallas_call | solution.py:341
  29.1 0.0 copy-start
  29.2 1.6 %copy-done = f32[1024,512]{1,0:T(8,128)S(1)} copy-done((f32[1024,512]{1,0:T(8,128)S(1)}, f32[1024,512]{1,0:T(8,128)}, u32[]{:S(2)}) %copy-start) | copy-done | bytes 2097176
  30.7 0.0 copy-start.1
  30.7 1.0 %copy-done.1 = bf16[192,1024]{1,0:T(8,128)(2,1)S(1)} copy-done((bf16[192,1024]{1,0:T(8,128)(2,1)S(1)}, bf16[192,1024]{1,0:T(8,128)(2,1)}, u32[]{:S(2)}) %copy-start.1) | copy-done | bytes 393240
  31.7 0.0 copy-start.3
  31.7 0.9 %copy-done.3 = bf16[192,512]{1,0:T(8,128)(2,1)S(1)} copy-done((bf16[192,512]{1,0:T(8,128)(2,1)S(1)}, bf16[192,512]{1,0:T(8,128)(2,1)}, u32[]{:S(2)}) %copy-start.3) | copy-done | bytes 196632
  32.7 0.0 copy-start.4
  32.7 0.7 copy-done.4
  33.3 0.0 copy-start.5
  33.3 0.7 copy-done.5
  34.0 0.0 copy-start.2
  34.0 14.6 %moments.1 = f32[66,192]{1,0:T(8,128)S(1)} custom-call(s32[120]{0:T(128)S(1)} %copy-done.5, s32[6]{0:T(128)S(1)} %copy-done.4, f32[1024,512]{1,0:T(8,128)S(1)} %copy-done, bf16[192,1024]{1,0:T(8,128)(2,1)S(1)} %copy-done.1, bf16[192,512]{1,0:T(8,128)(2,1)S(1)} %copy-done.3), custom_call_target="tpu_custom_call" | custom-call | tf_op jit(solution)/shard_map/moments/pallas_call | solution.py:181
  48.5 0.0 copy-done.6
  48.6 0.8 %fusion.x = f32[64,192]{1,0:T(8,128)} fusion(f32[64,66]{1,0:T(8,128)S(1)} %copy-done.6, f32[66,192]{1,0:T(8,128)S(1)} %moments.1), kind=kOutput, calls=%fused_computation | convolution fusion | flops 9732096 | bytes 116736 | tf_op jit(solution)/shard_map/dot_general | solution.py:472
  49.4 24.2 %total.1 = f32[64,192]{1,0:T(8,128)} custom-call(f32[64,192]{1,0:T(8,128)} %fusion.x), custom_call_target="tpu_custom_call" | custom-call | tf_op jit(solution)/shard_map/total/pallas_call | solution.py:445
  73.6 0.0 copy-done.2
  73.6 0.7 copy.11
  74.3 1.5 %copy.12 = f32[64,192]{1,0:T(8,128)} copy(f32[64,192]{1,0:T(8,128)} %total.1) | data formatting | bytes 98304
Async XLA Ops:
  2.4 46.2 %copy-start.6 = (f32[64,66]{1,0:T(8,128)S(1)}, f32[64,66]{1,0:T(8,128)}, u32[]{:S(2)}) copy-start(f32[64,66]{1,0:T(8,128)} %constant.8.clone) | copy-start | bytes 50692
  29.1 1.6 %copy-start = (f32[1024,512]{1,0:T(8,128)S(1)}, f32[1024,512]{1,0:T(8,128)}, u32[]{:S(2)}) copy-start(f32[1024,512]{1,0:T(8,128)} %cos_hbm.1) | copy-start | bytes 6291460
  30.7 1.0 %copy-start.1 = (bf16[192,1024]{1,0:T(8,128)(2,1)S(1)}, bf16[192,1024]{1,0:T(8,128)(2,1)}, u32[]{:S(2)}) copy-start(bf16[192,1024]{1,0:T(8,128)(2,1)} %get-tuple-element.4.ft) | copy-start | bytes 1179652
  31.7 0.9 %copy-start.3 = (bf16[192,512]{1,0:T(8,128)(2,1)S(1)}, bf16[192,512]{1,0:T(8,128)(2,1)}, u32[]{:S(2)}) copy-start(bf16[192,512]{1,0:T(8,128)(2,1)} %get-tuple-element.5.fct) | copy-start | bytes 589828
  32.7 0.7 copy-start.4
  33.3 0.7 copy-start.5
  34.0 39.6 %copy-start.2 = (bf16[192,1024]{1,0:T(8,128)(2,1)S(1)}, bf16[192,1024]{1,0:T(8,128)(2,1)}, u32[]{:S(2)}) copy-start(bf16[192,1024]{1,0:T(8,128)(2,1)} %get-tuple-element.4.ft) | copy-start | bytes 1179652

commit v2 on v1

v2 whole, which is shorter than its diff:
```python
import functools
import math

import jax
import jax.numpy as jnp
import numpy as np
from jax import lax
from jax.experimental import pallas as pl
from jax.experimental.pallas import tpu as pltpu
from jax.sharding import PartitionSpec as P

L = 64
LMIN = 2
TOP = LMIN + L - 1
LEVELS = TOP + 1
UNROLL = 6
TILE = 256
STRIP = 32
N_X = 4
LANES = 128
MESH = pl.DeviceIdType.MESH


def transform_matrix(npix):
    a = [math.comb(2 * k, k) / 4.0**k for k in range(TOP + 1)]
    out = np.zeros((-(-LEVELS // 8) * 8, LANES))
    for l in range(LMIN, TOP + 1):
        for k in range(l + 1):
            out[abs(l - 2 * k), l - LMIN] += a[k] * a[l - k] * (2 * l + 1) / npix
    return out.astype(np.float32)


def rank_order(rows, cols):
    spots = [(dz, dx) for dz in range(rows) for dx in range(cols) if dz or dx]
    reach = lambda d, n: min(d, n - d)
    return sorted(spots, key=lambda s: -(reach(s[0], rows) + reach(s[1], cols)))


LINE = [4, 5, 3, 2, 6, 1, 7]


def qml_kernel(
    n_rows, n_z, n_x,
    sky_hbm, cov_hbm, cos_hbm, matrix,
    filtered_out, spectra_out,
    sky, cov, cos, cheb, cheb_x, part, parcel, landed, rest, landed_rest, mine, rows, cols,
    lhs, lhs_x, fj, total, share, line_landed, line_sum, plane_landed, result,
    load_sem, send1, recv1, send_rest, recv_rest, send2, recv2, send3, recv3,
    send4, recv4, send5, recv5, send6, recv6,
):
    r = lax.axis_index("prow")
    c = lax.axis_index("pcol")
    n = n_z * n_x
    z, x = c // n_x, lax.rem(c, n_x)
    q, h = c // 2, lax.rem(c, 2)
    half_n = n // 2
    maps = sky.shape[1]
    per, width = parcel.shape[1], parcel.shape[2]
    order = rank_order(n_z, n_x)
    diagonal = r == q
    off = r != q
    side = jnp.where(r > q, h, 1 - h)
    barrier = pltpu.get_barrier_semaphore()

    def peer(spot):
        return lax.rem(z + spot[0], n_z) * n_x + lax.rem(x + spot[1], n_x)

    def line(e):
        return lax.rem(r + e, n_rows)

    def signal(device):
        pl.semaphore_signal(barrier, inc=1, device_id=device, device_id_type=MESH)

    def copy(src, dst, send, recv, device):
        return pltpu.make_async_remote_copy(
            src_ref=src, dst_ref=dst, send_sem=send, recv_sem=recv,
            device_id=device, device_id_type=MESH,
        )

    first = [jnp.where(diagonal, 2 * h, 2 * side), jnp.where(diagonal, 1 + 2 * h, 2 * side)]
    second = [jnp.where(diagonal, 2 * h + 1, 2 * side + 1), jnp.where(diagonal, 2 - 2 * h, 2 * side + 1)]
    spare = 2 - h

    def tile_at(index):
        return pl.ds(pl.multiple_of(index * TILE, TILE), TILE)

    loads = [
        pltpu.make_async_copy(sky_hbm, sky, load_sem.at[0]),
        pltpu.make_async_copy(cov_hbm, cov, load_sem.at[1]),
    ]
    for t in range(2):
        for s, row in enumerate((first[t], second[t])):
            loads.append(
                pltpu.make_async_copy(
                    cos_hbm.at[tile_at(row), pl.ds(t * TILE, TILE)],
                    cos.at[pl.ds((2 * t + s) * TILE, TILE)],
                    load_sem.at[2 + 2 * t + s],
                )
            )
    spare_load = pltpu.make_async_copy(
        cos_hbm.at[tile_at(spare), tile_at(h)], cos.at[pl.ds(4 * TILE, TILE)], load_sem.at[6]
    )
    for load in loads:
        load.start()

    @pl.when(diagonal)
    def _():
        spare_load.start()

    for spot in order:
        signal((r, peer(spot)))
    for e in LINE:
        signal((line(e), c))

    @pl.when(off)
    def _():
        for j in range(half_n):
            signal((q, h * half_n + j))

    loads[0].wait()
    loads[1].wait()
    sky_t = sky[...].astype(jnp.float32).T.astype(jnp.bfloat16)
    wide = 2 * width
    for g in range(cov.shape[0] // wide):
        value = lax.dot_general(
            sky_t, cov[g * wide : (g + 1) * wide, :], (((1,), (1,)), ((), ())),
            preferred_element_type=jnp.float32,
        )
        for a in range(2):
            for b in range(maps // per):
                k = (2 * g + a) * (maps // per) + b
                piece = value[b * per : (b + 1) * per, a * width : (a + 1) * width]
                part[k] = piece
                parcel[k] = piece.astype(jnp.bfloat16)

    pl.semaphore_wait(barrier, len(order) + 2 * (n_rows - 1))

    def scatter(s):
        to = peer(order[s])
        return copy(parcel.at[to], landed.at[s], send1.at[s], recv1.at[s], (r, to))

    for s in range(len(order)):
        scatter(s).start()

    def scatter_rest(j):
        to = h * half_n + j
        return copy(rest.at[j], landed_rest, send_rest.at[j], recv_rest, (r, to))

    @pl.when(diagonal)
    def _():
        for j in range(half_n):
            k = h * half_n + j
            rest[j] = (part[k] - parcel[k].astype(jnp.float32)).astype(jnp.bfloat16)
        for j in range(half_n):
            @pl.when(c != h * half_n + j)
            def _():
                scatter_rest(j).start()

    def generate(base, store):
        def strip(s, carry):
            at = pl.multiple_of(s * STRIP, STRIP)
            value = cos[pl.ds(base + at, STRIP), :]
            double = value + value
            before, now = value, jnp.ones_like(value)
            for k in range(LEVELS):
                store(k, at, now.astype(jnp.bfloat16))
                before, now = now, double * now - before
            return carry

        return strip

    def generate_pair(t):
        def store(k, at, value):
            cheb[k, t, pl.ds(at, STRIP), :] = value

        loads[2 + 2 * t].wait()
        loads[3 + 2 * t].wait()
        lax.fori_loop(0, 2 * TILE // STRIP, generate(2 * t * TILE, store), 0)

    generate_pair(0)

    sum_value = part[c]
    for s in range(len(order)):
        scatter(s).wait_recv()
        sum_value = sum_value + landed[s].astype(jnp.float32)
    part[c] = sum_value
    has_rest = c != 2 * r + c // half_n

    @pl.when(has_rest)
    def _():
        copy(rest.at[0], landed_rest, send_rest.at[0], recv_rest, (r, 2 * r + c // half_n)).wait_recv()
        part[c] = part[c] + landed_rest[...].astype(jnp.float32)

    mine[...] = part[c].astype(jnp.bfloat16)
    chunk_half = c // half_n

    def place(ref, k):
        return ref.at[
            pl.ds(pl.multiple_of(lax.rem(k, 2) * per, per), per),
            pl.ds(pl.multiple_of((k // 2) * width, width), width),
        ]

    def gather(s):
        return copy(mine, place(rows, c), send2.at[s], recv2.at[c], (r, peer(order[s])))

    def gathered(k):
        return copy(mine, place(rows, k), send2.at[0], recv2.at[k], (r, k))

    def column(e):
        return copy(
            mine, place(cols, lax.rem(c, half_n)), send3.at[e - 1], recv3.at[lax.rem(c, half_n)],
            (line(e), 2 * r + chunk_half),
        )

    def wanted(to):
        parity = jnp.where(to // 2 < r, chunk_half, 1 - chunk_half)
        return jnp.logical_or(to // 2 == r, lax.rem(to, 2) == parity)

    for e in LINE[:4]:
        column(e).start()
    for s in range(len(order)):
        @pl.when(wanted(peer(order[s])))
        def _():
            gather(s).start()
    for e in LINE[4:]:
        column(e).start()
    rows[
        pl.ds(pl.multiple_of(lax.rem(c, 2) * per, per), per),
        pl.ds(pl.multiple_of((c // 2) * width, width), width),
    ] = mine[...]

    generate_pair(1)

    @pl.when(diagonal)
    def _():
        def store(k, at, value):
            cheb_x[k, pl.ds(at, STRIP), :] = value

        spare_load.wait()
        lax.fori_loop(0, TILE // STRIP, generate(4 * TILE, store), 0)

    for s in range(len(order)):
        @pl.when(jnp.logical_not(wanted(peer(order[s]))))
        def _():
            gather(s).start()

    for k in range(n):
        needed = jnp.logical_or(diagonal, side == k // half_n)

        @pl.when(jnp.logical_and(needed, c != k))
        def _():
            gathered(k).wait_recv()

    @pl.when(off)
    def _():
        for j in range(half_n):
            copy(
                mine, place(cols, j), send3.at[0], recv3.at[j], (q, h * half_n + j)
            ).wait_recv()

    @pl.when(diagonal)
    def _():
        size = cols.shape[1]
        cols[...] = rows[:, pl.ds(pl.multiple_of(h * size, size), size)]

    weight = jnp.where(diagonal, 1, 2).astype(jnp.float32)
    for t in range(2):
        lhs[t, :, :TILE] = (rows[:, tile_at(first[t])].astype(jnp.float32) * weight).astype(jnp.bfloat16)
        lhs[t, :, TILE:] = (rows[:, tile_at(second[t])].astype(jnp.float32) * 2.0).astype(jnp.bfloat16)
        fj[t] = cols[:, t * TILE : (t + 1) * TILE].astype(jnp.float32)

    @pl.when(diagonal)
    def _():
        lhs_x[...] = (rows[:, tile_at(spare)].astype(jnp.float32) * 2.0).astype(jnp.bfloat16)

    total[...] = jnp.zeros_like(total)

    def levels(with_spare):
        def body(step, carry):
            acc = total[...]
            for u in range(UNROLL):
                k = step * UNROLL + u
                prod = None
                for t in range(2):
                    image = jnp.dot(lhs[t], cheb[k, t], preferred_element_type=jnp.float32)
                    term = image * fj[t]
                    prod = term if prod is None else prod + term
                if with_spare:
                    image = jnp.dot(lhs_x[...], cheb_x[k], preferred_element_type=jnp.float32)
                    prod = prod + image * fj[h]
                narrow = prod[:, :LANES] + prod[:, LANES:]
                moment = jnp.sum(narrow, axis=-1, keepdims=True)
                acc = acc + moment * matrix[pl.ds(k, 1), :]
            total[...] = acc
            return carry

        lax.fori_loop(0, LEVELS // UNROLL, body, 0)

    @pl.when(off)
    def _():
        levels(False)

    @pl.when(diagonal)
    def _():
        levels(True)

    share[...] = total[...].T[:L]

    piece = L // n_rows

    def block(k):
        return pl.ds(pl.multiple_of(k * piece, piece), piece)

    def reduce_line(e):
        return copy(
            share.at[block(line(e))], line_landed.at[e - 1], send4.at[e - 1], recv4.at[e - 1], (line(e), c)
        )

    def exchange(s):
        return copy(line_sum, plane_landed.at[c], send5.at[s], recv5.at[s], (r, peer(order[s])))

    def spread_line(e, k):
        return copy(result, spectra_out.at[block(k)], send6.at[e - 1], recv6.at[e - 1], (line(e), c))

    for e in LINE:
        reduce_line(e).start()

    for k in range(n):
        needed = jnp.logical_or(diagonal, side == k // half_n)

        @pl.when(jnp.logical_and(jnp.logical_not(needed), c != k))
        def _():
            gathered(k).wait_recv()

    def turn(g, carry):
        at = pl.ds(pl.multiple_of(g * LANES, LANES), LANES)
        filtered_out[at, :] = rows[:, at].astype(jnp.float32).T.astype(jnp.bfloat16)
        return carry

    lax.fori_loop(0, rows.shape[1] // LANES, turn, 0)

    for e in LINE:
        reduce_line(e).wait_recv()
    value = share[block(r)]
    for e in range(1, n_rows):
        value = value + line_landed[e - 1]
    line_sum[...] = value
    for s in range(len(order)):
        exchange(s).start()
    plane_landed[c] = value
    for s in range(len(order)):
        exchange(s).wait_recv()
    value = plane_landed[0]
    for k in range(1, n):
        value = value + plane_landed[k]
    result[...] = value
    for e in LINE:
        spread_line(e, r).start()
    spectra_out[block(r)] = value
    for e in LINE:
        spread_line(e, lax.rem(r - e + n_rows, n_rows)).wait_recv()

    for s in range(len(order)):
        scatter(s).wait_send()
        gather(s).wait_send()
        exchange(s).wait_send()
    for e in LINE:
        column(e).wait_send()
        reduce_line(e).wait_send()
        spread_line(e, r).wait_send()

    @pl.when(diagonal)
    def _():
        for j in range(half_n):
            @pl.when(c != h * half_n + j)
            def _():
                scatter_rest(j).wait_send()


def per_device(npix, n_rows, n_cols, inverse_cov, cosines, sky_maps):
    n_z = n_cols // N_X
    n = n_cols
    size, cols_here = inverse_cov.shape
    maps = sky_maps.shape[1]
    per, width = maps // 2, 2 * size // n
    piece = L // n_rows
    vmem = pl.BlockSpec(memory_space=pltpu.VMEM)
    anywhere = pl.BlockSpec(memory_space=pl.ANY)
    bf16, f32 = jnp.bfloat16, jnp.float32
    plane = pltpu.SemaphoreType.DMA((n - 1,))
    line = pltpu.SemaphoreType.DMA((n_rows - 1,))
    half = pltpu.SemaphoreType.DMA((n // 2,))
    filtered, spectra = pl.pallas_call(
        functools.partial(qml_kernel, n_rows, n_z, N_X),
        out_shape=(
            jax.ShapeDtypeStruct((size, maps), bf16),
            jax.ShapeDtypeStruct((L, maps), f32),
        ),
        in_specs=[anywhere, anywhere, anywhere, vmem],
        out_specs=(vmem, vmem),
        scratch_shapes=[
            pltpu.VMEM(sky_maps.shape, bf16),
            pltpu.VMEM(inverse_cov.shape, bf16),
            pltpu.VMEM((5 * TILE, TILE), f32),
            pltpu.VMEM((LEVELS, 2, 2 * TILE, TILE), bf16),
            pltpu.VMEM((LEVELS, TILE, TILE), bf16),
            pltpu.VMEM((n, per, width), f32),
            pltpu.VMEM((n, per, width), bf16),
            pltpu.VMEM((n - 1, per, width), bf16),
            pltpu.VMEM((n // 2, per, width), bf16),
            pltpu.VMEM((per, width), bf16),
            pltpu.VMEM((per, width), bf16),
            pltpu.VMEM((maps, size), bf16),
            pltpu.VMEM((maps, cols_here), bf16),
            pltpu.VMEM((2, maps, 2 * TILE), bf16),
            pltpu.VMEM((maps, TILE), bf16),
            pltpu.VMEM((2, maps, TILE), f32),
            pltpu.VMEM((maps, LANES), f32),
            pltpu.VMEM((L, maps), f32),
            pltpu.VMEM((n_rows - 1, piece, maps), f32),
            pltpu.VMEM((piece, maps), f32),
            pltpu.VMEM((n, piece, maps), f32),
            pltpu.VMEM((piece, maps), f32),
            pltpu.SemaphoreType.DMA((7,)),
            plane, plane, half, pltpu.SemaphoreType.DMA, plane, pltpu.SemaphoreType.DMA((n,)),
            line, half, line, line, plane, plane, line, line,
        ],
        compiler_params=pltpu.CompilerParams(
            collective_id=1, has_side_effects=True, vmem_limit_bytes=60 * 2**20
        ),
        name="qml",
    )(sky_maps, inverse_cov, cosines, jnp.asarray(transform_matrix(npix)))
    return filtered, spectra


def solution(mesh):
    in_specs = (P("prow", "pcol"), P("prow", "pcol"), P("pcol", None))
    out_specs = (P("prow", None), P())
    n_rows, n_cols = mesh.shape["prow"], mesh.shape["pcol"]

    def whole(inverse_cov, cosines, sky_maps):
        npix = cosines.shape[0]
        step = jax.shard_map(
            functools.partial(per_device, npix, n_rows, n_cols),
            mesh=mesh, in_specs=in_specs, out_specs=out_specs, check_vma=False,
        )
        return step(inverse_cov, cosines, sky_maps)

    return whole
```

time: 76.2 us -> 58.7 us (0.77)
  Pallas kernels: 65.5 us -> 52.5 us
  local copies, waits for them, and re-layouts: 8.81 us -> 5.22 us
  matrix products: 0.83 us -> 0 us
    pallas_call x3 -> x1, Pallas kernels: 65.5 us -> 52.5 us  [per_device(): pl.pallas_call(functools.partial(qml_kernel, n_rows, n_z, N_X), out_shape...]
    unnamed x17 -> x2, local copies, waits for them, and re-layouts: 8.81 us -> 3.24 us
    pallas_call x0 -> x1, local copies, waits for them, and re-layouts: none -> 1.98 us  [per_device(): pl.pallas_call(functools.partial(qml_kernel, n_rows, n_z, N_X), out_shape...]
    dot_general x1 -> x0, matrix products: 0.83 us -> none  [per_device(): jnp.dot(jnp.asarray(matrix), moments, precision=lax.Precision.HIGHEST)]
where the time goes in v2:
time: 58.7 us; the launch traced here: 58.4 us
  Pallas kernels  52.5 us (89%)
  local copies, waits for them, and re-layouts  5.22 us (9%)
  between operations  0.64 us (1%)
    pallas_call x1, Pallas kernels, per_device(): pl.pallas_call(functools.partial(qml_kernel, n_rows, n_z, N_X), out_shape...  52.5 us
    unnamed x2, local copies, waits for them, and re-layouts  3.24 us
    pallas_call x1, local copies, waits for them, and re-layouts, per_device(): pl.pallas_call(functools.partial(qml_kernel, n_rows, n_z, N_X), out_shape...  1.98 us

profile of v2, /device:TPU:1, one launch (start us, length us, event | category | flops | bytes accessed | tf_op | source)
XLA Modules:
  0.0 58.4 jit_solution(16103936069431297828)
XLA Ops:
  0.6 1.8 %copy.6.sky_hbm = bf16[512,192]{1,0:T(8,128)(2,1)} copy(bf16[512,192]{0,1:T(8,128)(2,1)} %param.6) | data formatting | bytes 393216 | tf_op args[2]
  2.4 52.5 %qml.1 = (bf16[1024,192]{1,0:T(8,128)(2,1)}, f32[64,192]{1,0:T(8,128)}) custom-call(bf16[512,192]{1,0:T(8,128)(2,1)} %copy.6.sky_hbm, bf16[1024,512]{1,0:T(8,128)(2,1)} %cov_hbm.1, f32[1024,512]{1,0:T(8,128)} %cos_hbm.1, f32[72,128]{1,0:T(8,128)} %constant.2.clone.matrix), custom_call_target="tpu_custom_call" | custom-call | tf_op jit(solution)/shard_map/qml/pallas_call | solution.py:393
  54.9 2.0 %copy.7 = bf16[1024,192]{0,1:T(8,128)(2,1)} copy(bf16[1024,192]{1,0:T(8,128)(2,1)} %get-tuple-element.2) | data formatting | bytes 786432 | tf_op jit(solution)/shard_map/qml/pallas_call | solution.py:393
  56.9 1.5 %copy.9 = f32[64,192]{1,0:T(8,128)} copy(f32[64,192]{1,0:T(8,128)} %get-tuple-element.7) | data formatting | bytes 98304

commit v3 on v2

--- a/solution.py
+++ b/solution.py
@@ -41,9 +41,9 @@
 
 def qml_kernel(
     n_rows, n_z, n_x,
-    sky_hbm, cov_hbm, cos_hbm, matrix,
-    filtered_out, spectra_out,
-    sky, cov, cos, cheb, cheb_x, part, parcel, landed, rest, landed_rest, mine, rows, cols,
+    sky_hbm, cov_hbm, cos_hbm, matrix_hbm,
+    rows, spectra_out,
+    sky, cov, cos, matrix, cheb, cheb_x, part, parcel, landed, rest, landed_rest, mine, cols,
     lhs, lhs_x, fj, total, share, line_landed, line_sum, plane_landed, result,
     load_sem, send1, recv1, send_rest, recv_rest, send2, recv2, send3, recv3,
     send4, recv4, send5, recv5, send6, recv6,
@@ -54,7 +54,7 @@
     z, x = c // n_x, lax.rem(c, n_x)
     q, h = c // 2, lax.rem(c, 2)
     half_n = n // 2
-    maps = sky.shape[1]
+    maps = sky.shape[0]
     per, width = parcel.shape[1], parcel.shape[2]
     order = rank_order(n_z, n_x)
     diagonal = r == q
@@ -97,11 +97,13 @@
                     load_sem.at[2 + 2 * t + s],
                 )
             )
+    matrix_load = pltpu.make_async_copy(matrix_hbm, matrix, load_sem.at[7])
     spare_load = pltpu.make_async_copy(
         cos_hbm.at[tile_at(spare), tile_at(h)], cos.at[pl.ds(4 * TILE, TILE)], load_sem.at[6]
     )
     for load in loads:
         load.start()
+    matrix_load.start()
 
     @pl.when(diagonal)
     def _():
@@ -119,11 +121,10 @@
 
     loads[0].wait()
     loads[1].wait()
-    sky_t = sky[...].astype(jnp.float32).T.astype(jnp.bfloat16)
     wide = 2 * width
     for g in range(cov.shape[0] // wide):
         value = lax.dot_general(
-            sky_t, cov[g * wide : (g + 1) * wide, :], (((1,), (1,)), ((), ())),
+            sky[...], cov[g * wide : (g + 1) * wide, :], (((1,), (1,)), ((), ())),
             preferred_element_type=jnp.float32,
         )
         for a in range(2):
@@ -273,6 +274,7 @@
     def _():
         lhs_x[...] = (rows[:, tile_at(spare)].astype(jnp.float32) * 2.0).astype(jnp.bfloat16)
 
+    matrix_load.wait()
     total[...] = jnp.zeros_like(total)
 
     def levels(with_spare):
@@ -332,13 +334,6 @@
         def _():
             gathered(k).wait_recv()
 
-    def turn(g, carry):
-        at = pl.ds(pl.multiple_of(g * LANES, LANES), LANES)
-        filtered_out[at, :] = rows[:, at].astype(jnp.float32).T.astype(jnp.bfloat16)
-        return carry
-
-    lax.fori_loop(0, rows.shape[1] // LANES, turn, 0)
-
     for e in LINE:
         reduce_line(e).wait_recv()
     value = share[block(r)]
@@ -382,10 +377,13 @@
     n = n_cols
     size, cols_here = inverse_cov.shape
     maps = sky_maps.shape[1]
+    sky_t = sky_maps.T
     per, width = maps // 2, 2 * size // n
     piece = L // n_rows
     vmem = pl.BlockSpec(memory_space=pltpu.VMEM)
-    anywhere = pl.BlockSpec(memory_space=pl.ANY)
+    hbm = pl.BlockSpec(memory_space=pltpu.HBM)
+    matrix = jnp.asarray(transform_matrix(npix))
+    inputs = (sky_t, inverse_cov, cosines, matrix)
     bf16, f32 = jnp.bfloat16, jnp.float32
     plane = pltpu.SemaphoreType.DMA((n - 1,))
     line = pltpu.SemaphoreType.DMA((n_rows - 1,))
@@ -393,15 +391,16 @@
     filtered, spectra = pl.pallas_call(
         functools.partial(qml_kernel, n_rows, n_z, N_X),
         out_shape=(
-            jax.ShapeDtypeStruct((size, maps), bf16),
+            jax.ShapeDtypeStruct((maps, size), bf16),
             jax.ShapeDtypeStruct((L, maps), f32),
         ),
-        in_specs=[anywhere, anywhere, anywhere, vmem],
+        in_specs=[hbm] * len(inputs),
         out_specs=(vmem, vmem),
         scratch_shapes=[
-            pltpu.VMEM(sky_maps.shape, bf16),
+            pltpu.VMEM(sky_t.shape, bf16),
             pltpu.VMEM(inverse_cov.shape, bf16),
             pltpu.VMEM((5 * TILE, TILE), f32),
+            pltpu.VMEM(matrix.shape, f32),
             pltpu.VMEM((LEVELS, 2, 2 * TILE, TILE), bf16),
             pltpu.VMEM((LEVELS, TILE, TILE), bf16),
             pltpu.VMEM((n, per, width), f32),
@@ -410,7 +409,6 @@
             pltpu.VMEM((n // 2, per, width), bf16),
             pltpu.VMEM((per, width), bf16),
             pltpu.VMEM((per, width), bf16),
-            pltpu.VMEM((maps, size), bf16),
             pltpu.VMEM((maps, cols_here), bf16),
             pltpu.VMEM((2, maps, 2 * TILE), bf16),
             pltpu.VMEM((maps, TILE), bf16),
@@ -421,16 +419,16 @@
             pltpu.VMEM((piece, maps), f32),
             pltpu.VMEM((n, piece, maps), f32),
             pltpu.VMEM((piece, maps), f32),
-            pltpu.SemaphoreType.DMA((7,)),
+            pltpu.SemaphoreType.DMA((8,)),
             plane, plane, half, pltpu.SemaphoreType.DMA, plane, pltpu.SemaphoreType.DMA((n,)),
             line, half, line, line, plane, plane, line, line,
         ],
         compiler_params=pltpu.CompilerParams(
-            collective_id=1, has_side_effects=True, vmem_limit_bytes=60 * 2**20
+            collective_id=1, has_side_effects=True, vmem_limit_bytes=50 * 2**20
         ),
         name="qml",
-    )(sky_maps, inverse_cov, cosines, jnp.asarray(transform_matrix(npix)))
-    return filtered, spectra
+    )(*[pltpu.with_memory_space_constraint(value, pltpu.HBM) for value in inputs])
+    return filtered.T, spectra
 
 
 def solution(mesh):

time: 58.7 us -> 53.5 us (0.911)
  local copies, waits for them, and re-layouts: 5.22 us -> 1.38 us
  Pallas kernels: 52.5 us -> 51.3 us
    pallas_call x1 -> x0, local copies, waits for them, and re-layouts: 1.98 us -> none  [per_device(): pl.pallas_call(functools.partial(qml_kernel, n_rows, n_z, N_X), out_shape...]
    unnamed x2, local copies, waits for them, and re-layouts: 3.24 us -> 1.38 us
    pallas_call x1, Pallas kernels: 52.5 us -> 51.3 us  [per_device(): pl.pallas_call(functools.partial(qml_kernel, n_rows, n_z, N_X), out_shape...]
where the time goes in v3:
time: 53.5 us; the launch traced here: 53.4 us
  Pallas kernels  51.3 us (96%)
  local copies, waits for them, and re-layouts  1.38 us (3%)
  between operations  0.64 us (1%)
    pallas_call x1, Pallas kernels, per_device(): pl.pallas_call(functools.partial(qml_kernel, n_rows, n_z, N_X), out_shape...  51.3 us
    unnamed x2, local copies, waits for them, and re-layouts  1.38 us

profile of v3, /device:TPU:1, one launch (start us, length us, event | category | flops | bytes accessed | tf_op | source)
XLA Modules:
  0.0 53.4 jit_solution(2344664598716682423)
XLA Ops:
  0.6 51.3 %qml.1 = (bf16[192,1024]{1,0:T(8,128)(2,1)S(1)}, f32[64,192]{1,0:T(8,128)S(1)}) custom-call(bf16[192,512]{1,0:T(8,128)(2,1)} %bitcast.3, bf16[1024,512]{1,0:T(8,128)(2,1)} %cov_hbm.1, f32[1024,512]{1,0:T(8,128)} %cos_hbm.1, f32[72,128]{1,0:T(8,128)} %constant.2.clone.matrix_hbm), custom_call_target="tpu_custom_call" | custom-call | tf_op jit(solution)/shard_map/qml/pallas_call | solution.py:391
  52.0 0.7 %copy.8 = bf16[1024,192]{0,1:T(8,128)(2,1)} copy(bf16[1024,192]{0,1:T(8,128)(2,1)S(1)} %bitcast.2) | data formatting | bytes 786432
  52.7 0.6 %copy.9 = f32[64,192]{1,0:T(8,128)} copy(f32[64,192]{1,0:T(8,128)S(1)} %get-tuple-element.9) | data formatting | bytes 98304

commit v4 on v3

--- a/solution.py
+++ b/solution.py
@@ -13,7 +13,7 @@
 LMIN = 2
 TOP = LMIN + L - 1
 LEVELS = TOP + 1
-UNROLL = 6
+UNROLL = 22
 TILE = 256
 STRIP = 32
 N_X = 4
@@ -68,6 +68,17 @@
     def line(e):
         return lax.rem(r + e, n_rows)
 
+    def turn(row):
+        return n_x // 2 * lax.rem(row, 2) + n_x - 1
+
+    def chunk_of(row, col):
+        return lax.rem(lax.rem(col, n_x) - turn(row) + 2 * n_x, n_x) * n_z + col // n_x
+
+    def owner(row, k):
+        return (k % n_z if isinstance(k, int) else lax.rem(k, n_z)) * n_x + lax.rem(k // n_z + turn(row), n_x)
+
+    me = chunk_of(r, c)
+
     def signal(device):
         pl.semaphore_signal(barrier, inc=1, device_id=device, device_id_type=MESH)
 
@@ -117,7 +128,7 @@
     @pl.when(off)
     def _():
         for j in range(half_n):
-            signal((q, h * half_n + j))
+            signal((q, owner(q, h * half_n + j)))
 
     loads[0].wait()
     loads[1].wait()
@@ -138,13 +149,13 @@
 
     def scatter(s):
         to = peer(order[s])
-        return copy(parcel.at[to], landed.at[s], send1.at[s], recv1.at[s], (r, to))
+        return copy(parcel.at[chunk_of(r, to)], landed.at[s], send1.at[s], recv1.at[s], (r, to))
 
     for s in range(len(order)):
         scatter(s).start()
 
     def scatter_rest(j):
-        to = h * half_n + j
+        to = owner(r, h * half_n + j)
         return copy(rest.at[j], landed_rest, send_rest.at[j], recv_rest, (r, to))
 
     @pl.when(diagonal)
@@ -153,7 +164,7 @@
             k = h * half_n + j
             rest[j] = (part[k] - parcel[k].astype(jnp.float32)).astype(jnp.bfloat16)
         for j in range(half_n):
-            @pl.when(c != h * half_n + j)
+            @pl.when(me != h * half_n + j)
             def _():
                 scatter_rest(j).start()
 
@@ -180,20 +191,20 @@
 
     generate_pair(0)
 
-    sum_value = part[c]
+    sum_value = part[me]
     for s in range(len(order)):
         scatter(s).wait_recv()
         sum_value = sum_value + landed[s].astype(jnp.float32)
-    part[c] = sum_value
-    has_rest = c != 2 * r + c // half_n
+    part[me] = sum_value
+    chunk_half = me // half_n
+    has_rest = c != 2 * r + chunk_half
 
     @pl.when(has_rest)
     def _():
-        copy(rest.at[0], landed_rest, send_rest.at[0], recv_rest, (r, 2 * r + c // half_n)).wait_recv()
-        part[c] = part[c] + landed_rest[...].astype(jnp.float32)
-
-    mine[...] = part[c].astype(jnp.bfloat16)
-    chunk_half = c // half_n
+        copy(rest.at[0], landed_rest, send_rest.at[0], recv_rest, (r, 2 * r + chunk_half)).wait_recv()
+        part[me] = part[me] + landed_rest[...].astype(jnp.float32)
+
+    mine[...] = part[me].astype(jnp.bfloat16)
 
     def place(ref, k):
         return ref.at[
@@ -202,14 +213,14 @@
         ]
 
     def gather(s):
-        return copy(mine, place(rows, c), send2.at[s], recv2.at[c], (r, peer(order[s])))
+        return copy(mine, place(rows, me), send2.at[s], recv2.at[me], (r, peer(order[s])))
 
     def gathered(k):
-        return copy(mine, place(rows, k), send2.at[0], recv2.at[k], (r, k))
+        return copy(mine, place(rows, k), send2.at[0], recv2.at[k], (r, owner(r, k)))
 
     def column(e):
         return copy(
-            mine, place(cols, lax.rem(c, half_n)), send3.at[e - 1], recv3.at[lax.rem(c, half_n)],
+            mine, place(cols, lax.rem(me, half_n)), send3.at[e - 1], recv3.at[lax.rem(me, half_n)],
             (line(e), 2 * r + chunk_half),
         )
 
@@ -226,8 +237,8 @@
     for e in LINE[4:]:
         column(e).start()
     rows[
-        pl.ds(pl.multiple_of(lax.rem(c, 2) * per, per), per),
-        pl.ds(pl.multiple_of((c // 2) * width, width), width),
+        pl.ds(pl.multiple_of(lax.rem(me, 2) * per, per), per),
+        pl.ds(pl.multiple_of((me // 2) * width, width), width),
     ] = mine[...]
 
     generate_pair(1)
@@ -248,7 +259,7 @@
     for k in range(n):
         needed = jnp.logical_or(diagonal, side == k // half_n)
 
-        @pl.when(jnp.logical_and(needed, c != k))
+        @pl.when(jnp.logical_and(needed, me != k))
         def _():
             gathered(k).wait_recv()
 
@@ -256,7 +267,7 @@
     def _():
         for j in range(half_n):
             copy(
-                mine, place(cols, j), send3.at[0], recv3.at[j], (q, h * half_n + j)
+                mine, place(cols, j), send3.at[0], recv3.at[j], (q, owner(q, h * half_n + j))
             ).wait_recv()
 
     @pl.when(diagonal)
@@ -330,7 +341,7 @@
     for k in range(n):
         needed = jnp.logical_or(diagonal, side == k // half_n)
 
-        @pl.when(jnp.logical_and(jnp.logical_not(needed), c != k))
+        @pl.when(jnp.logical_and(jnp.logical_not(needed), me != k))
         def _():
             gathered(k).wait_recv()
 
@@ -367,7 +378,7 @@
     @pl.when(diagonal)
     def _():
         for j in range(half_n):
-            @pl.when(c != h * half_n + j)
+            @pl.when(me != h * half_n + j)
             def _():
                 scatter_rest(j).wait_send()
 

time: 53.5 us -> 49.4 us (0.923)
  Pallas kernels: 51.3 us -> 47.2 us
    pallas_call x1, Pallas kernels: 51.3 us -> 47.2 us  [per_device(): pl.pallas_call(functools.partial(qml_kernel, n_rows, n_z, N_X), out_shape...]
where the time goes in v4:
time: 49.4 us; the launch traced here: 49.2 us
  Pallas kernels  47.2 us (96%)
  local copies, waits for them, and re-layouts  1.38 us (3%)
  between operations  0.64 us (1%)
    pallas_call x1, Pallas kernels, per_device(): pl.pallas_call(functools.partial(qml_kernel, n_rows, n_z, N_X), out_shape...  47.2 us
    unnamed x2, local copies, waits for them, and re-layouts  1.38 us

profile of v4, /device:TPU:1, one launch (start us, length us, event | category | flops | bytes accessed | tf_op | source)
XLA Modules:
  0.0 49.2 jit_solution(17151877163461271608)
XLA Ops:
  0.6 47.2 %qml.1 = (bf16[192,1024]{1,0:T(8,128)(2,1)S(1)}, f32[64,192]{1,0:T(8,128)S(1)}) custom-call(bf16[192,512]{1,0:T(8,128)(2,1)} %bitcast.3, bf16[1024,512]{1,0:T(8,128)(2,1)} %cov_hbm.1, f32[1024,512]{1,0:T(8,128)} %cos_hbm.1, f32[72,128]{1,0:T(8,128)} %constant.2.clone.matrix_hbm), custom_call_target="tpu_custom_call" | custom-call | tf_op jit(solution)/shard_map/qml/pallas_call | solution.py:402
  47.9 0.7 %copy.8 = bf16[1024,192]{0,1:T(8,128)(2,1)} copy(bf16[1024,192]{0,1:T(8,128)(2,1)S(1)} %bitcast.2) | data formatting | bytes 786432
  48.6 0.6 %copy.9 = f32[64,192]{1,0:T(8,128)} copy(f32[64,192]{1,0:T(8,128)S(1)} %get-tuple-element.9) | data formatting | bytes 98304

commit v5 on v4

--- a/solution.py
+++ b/solution.py
@@ -14,9 +14,12 @@
 TOP = LMIN + L - 1
 LEVELS = TOP + 1
 UNROLL = 22
+HALF = LEVELS // 2
+SPARE_UNROLL = 33
 TILE = 256
 STRIP = 32
 N_X = 4
+PARTS = 2
 LANES = 128
 MESH = pl.DeviceIdType.MESH
 
@@ -44,9 +47,9 @@
     sky_hbm, cov_hbm, cos_hbm, matrix_hbm,
     rows, spectra_out,
     sky, cov, cos, matrix, cheb, cheb_x, part, parcel, landed, rest, landed_rest, mine, cols,
-    lhs, lhs_x, fj, total, share, line_landed, line_sum, plane_landed, result,
+    lhs, lhs_x, rows_x, fj, total, share, line_landed, line_sum, plane_landed, result,
     load_sem, send1, recv1, send_rest, recv_rest, send2, recv2, send3, recv3,
-    send4, recv4, send5, recv5, send6, recv6,
+    send4, recv4, send5, recv5, send6, recv6, send_x, recv_x,
 ):
     r = lax.axis_index("prow")
     c = lax.axis_index("pcol")
@@ -59,6 +62,8 @@
     order = rank_order(n_z, n_x)
     diagonal = r == q
     off = r != q
+    partner = r + 1 - 2 * lax.rem(r, 2)
+    helper = partner == q
     side = jnp.where(r > q, h, 1 - h)
     barrier = pltpu.get_barrier_semaphore()
 
@@ -112,13 +117,8 @@
     spare_load = pltpu.make_async_copy(
         cos_hbm.at[tile_at(spare), tile_at(h)], cos.at[pl.ds(4 * TILE, TILE)], load_sem.at[6]
     )
-    for load in loads:
+    for load in loads[:2]:
         load.start()
-    matrix_load.start()
-
-    @pl.when(diagonal)
-    def _():
-        spare_load.start()
 
     for spot in order:
         signal((r, peer(spot)))
@@ -132,6 +132,14 @@
 
     loads[0].wait()
     loads[1].wait()
+    for load in loads[2:]:
+        load.start()
+    matrix_load.start()
+
+    @pl.when(diagonal)
+    def _():
+        spare_load.start()
+
     wide = 2 * width
     for g in range(cov.shape[0] // wide):
         value = lax.dot_general(
@@ -147,34 +155,55 @@
 
     pl.semaphore_wait(barrier, len(order) + 2 * (n_rows - 1))
 
-    def scatter(s):
+    def part_of(ref, p):
+        return ref.at[pl.ds(p * (per // PARTS), per // PARTS)]
+
+    def scatter(s, p):
         to = peer(order[s])
-        return copy(parcel.at[chunk_of(r, to)], landed.at[s], send1.at[s], recv1.at[s], (r, to))
+        return copy(
+            part_of(parcel.at[chunk_of(r, to)], p), part_of(landed.at[s], p),
+            send1.at[s], recv1.at[PARTS * s + p], (r, to),
+        )
+
+    def scatter_rest(j, p):
+        to = owner(r, h * half_n + j)
+        return copy(part_of(rest.at[j], p), part_of(landed_rest, p), send_rest.at[j], recv_rest.at[p], (r, to))
+
+    def spare_cos():
+        tile = cos.at[pl.ds(4 * TILE, TILE)]
+        return copy(tile, tile, send_x.at[0], recv_x.at[0], (partner, c))
+
+    def spare_rows():
+        return copy(rows.at[:, tile_at(spare)], rows_x, send_x.at[1], recv_x.at[1], (partner, c))
 
     for s in range(len(order)):
-        scatter(s).start()
-
-    def scatter_rest(j):
-        to = owner(r, h * half_n + j)
-        return copy(rest.at[j], landed_rest, send_rest.at[j], recv_rest, (r, to))
+        scatter(s, 0).start()
 
     @pl.when(diagonal)
     def _():
         for j in range(half_n):
             k = h * half_n + j
             rest[j] = (part[k] - parcel[k].astype(jnp.float32)).astype(jnp.bfloat16)
-        for j in range(half_n):
-            @pl.when(me != h * half_n + j)
-            def _():
-                scatter_rest(j).start()
-
-    def generate(base, store):
+
+    for p in range(PARTS):
+        @pl.when(diagonal)
+        def _():
+            for j in range(half_n):
+                @pl.when(me != h * half_n + j)
+                def _():
+                    scatter_rest(j, p).start()
+
+        if p + 1 < PARTS:
+            for s in range(len(order)):
+                scatter(s, p + 1).start()
+
+    def generate(base, store, count=LEVELS):
         def strip(s, carry):
             at = pl.multiple_of(s * STRIP, STRIP)
             value = cos[pl.ds(base + at, STRIP), :]
             double = value + value
             before, now = value, jnp.ones_like(value)
-            for k in range(LEVELS):
+            for k in range(count):
                 store(k, at, now.astype(jnp.bfloat16))
                 before, now = now, double * now - before
             return carry
@@ -189,22 +218,15 @@
         loads[3 + 2 * t].wait()
         lax.fori_loop(0, 2 * TILE // STRIP, generate(2 * t * TILE, store), 0)
 
+    @pl.when(diagonal)
+    def _():
+        spare_load.wait()
+        spare_cos().start()
+
     generate_pair(0)
 
-    sum_value = part[me]
-    for s in range(len(order)):
-        scatter(s).wait_recv()
-        sum_value = sum_value + landed[s].astype(jnp.float32)
-    part[me] = sum_value
     chunk_half = me // half_n
     has_rest = c != 2 * r + chunk_half
-
-    @pl.when(has_rest)
-    def _():
-        copy(rest.at[0], landed_rest, send_rest.at[0], recv_rest, (r, 2 * r + chunk_half)).wait_recv()
-        part[me] = part[me] + landed_rest[...].astype(jnp.float32)
-
-    mine[...] = part[me].astype(jnp.bfloat16)
 
     def place(ref, k):
         return ref.at[
@@ -212,15 +234,15 @@
             pl.ds(pl.multiple_of((k // 2) * width, width), width),
         ]
 
-    def gather(s):
-        return copy(mine, place(rows, me), send2.at[s], recv2.at[me], (r, peer(order[s])))
+    def gather(s, cut=lambda ref: ref):
+        return copy(cut(mine), cut(place(rows, me)), send2.at[s], recv2.at[me], (r, peer(order[s])))
 
     def gathered(k):
         return copy(mine, place(rows, k), send2.at[0], recv2.at[k], (r, owner(r, k)))
 
-    def column(e):
+    def column(e, cut=lambda ref: ref):
         return copy(
-            mine, place(cols, lax.rem(me, half_n)), send3.at[e - 1], recv3.at[lax.rem(me, half_n)],
+            cut(mine), cut(place(cols, lax.rem(me, half_n))), send3.at[e - 1], recv3.at[lax.rem(me, half_n)],
             (line(e), 2 * r + chunk_half),
         )
 
@@ -228,14 +250,32 @@
         parity = jnp.where(to // 2 < r, chunk_half, 1 - chunk_half)
         return jnp.logical_or(to // 2 == r, lax.rem(to, 2) == parity)
 
-    for e in LINE[:4]:
-        column(e).start()
-    for s in range(len(order)):
-        @pl.when(wanted(peer(order[s])))
+    for p in range(PARTS):
+        cut = functools.partial(part_of, p=p)
+        span = slice(p * (per // PARTS), (p + 1) * (per // PARTS))
+        sum_value = part[me, span]
+        for s in range(len(order)):
+            scatter(s, p).wait_recv()
+            sum_value = sum_value + landed[s, span].astype(jnp.float32)
+        part[me, span] = sum_value
+
+        @pl.when(has_rest)
         def _():
-            gather(s).start()
-    for e in LINE[4:]:
-        column(e).start()
+            copy(
+                part_of(rest.at[0], p), part_of(landed_rest, p), send_rest.at[0], recv_rest.at[p],
+                (r, 2 * r + chunk_half),
+            ).wait_recv()
+            part[me, span] = part[me, span] + landed_rest[span].astype(jnp.float32)
+
+        mine[span] = part[me, span].astype(jnp.bfloat16)
+        for e in LINE[:4]:
+            column(e, cut).start()
+        for s in range(len(order)):
+            @pl.when(wanted(peer(order[s])))
+            def _():
+                gather(s, cut).start()
+        for e in LINE[4:]:
+            column(e, cut).start()
     rows[
         pl.ds(pl.multiple_of(lax.rem(me, 2) * per, per), per),
         pl.ds(pl.multiple_of((me // 2) * width, width), width),
@@ -246,10 +286,18 @@
     @pl.when(diagonal)
     def _():
         def store(k, at, value):
+            if k >= HALF:
+                cheb_x[k - HALF, pl.ds(at, STRIP), :] = value
+
+        lax.fori_loop(0, TILE // STRIP, generate(4 * TILE, store), 0)
+
+    @pl.when(helper)
+    def _():
+        def store(k, at, value):
             cheb_x[k, pl.ds(at, STRIP), :] = value
 
-        spare_load.wait()
-        lax.fori_loop(0, TILE // STRIP, generate(4 * TILE, store), 0)
+        spare_cos().wait_recv()
+        lax.fori_loop(0, TILE // STRIP, generate(4 * TILE, store, HALF), 0)
 
     for s in range(len(order)):
         @pl.when(jnp.logical_not(wanted(peer(order[s]))))
@@ -272,6 +320,7 @@
 
     @pl.when(diagonal)
     def _():
+        spare_rows().start()
         size = cols.shape[1]
         cols[...] = rows[:, pl.ds(pl.multiple_of(h * size, size), size)]
 
@@ -281,41 +330,51 @@
         lhs[t, :, TILE:] = (rows[:, tile_at(second[t])].astype(jnp.float32) * 2.0).astype(jnp.bfloat16)
         fj[t] = cols[:, t * TILE : (t + 1) * TILE].astype(jnp.float32)
 
-    @pl.when(diagonal)
-    def _():
-        lhs_x[...] = (rows[:, tile_at(spare)].astype(jnp.float32) * 2.0).astype(jnp.bfloat16)
-
     matrix_load.wait()
     total[...] = jnp.zeros_like(total)
 
-    def levels(with_spare):
-        def body(step, carry):
+    def add_moment(acc, prod, k):
+        narrow = prod[:, :LANES] + prod[:, LANES:]
+        return acc + jnp.sum(narrow, axis=-1, keepdims=True) * matrix[pl.ds(k, 1), :]
+
+    def level_step(step, carry):
+        acc = total[...]
+        for u in range(UNROLL):
+            k = step * UNROLL + u
+            prod = None
+            for t in range(2):
+                image = jnp.dot(lhs[t], cheb[k, t], preferred_element_type=jnp.float32)
+                term = image * fj[t]
+                prod = term if prod is None else prod + term
+            acc = add_moment(acc, prod, k)
+        total[...] = acc
+        return carry
+
+    lax.fori_loop(0, LEVELS // UNROLL, level_step, 0)
+
+    @pl.when(diagonal)
+    def _():
+        lhs_x[...] = (rows[:, tile_at(spare)].astype(jnp.float32) * 2.0).astype(jnp.bfloat16)
+
+    @pl.when(helper)
+    def _():
+        spare_rows().wait_recv()
+        lhs_x[...] = (rows_x[...].astype(jnp.float32) * 2.0).astype(jnp.bfloat16)
+
+    @pl.when(jnp.logical_or(diagonal, helper))
+    def _():
+        base = jnp.where(diagonal, HALF, 0)
+
+        def spare_step(step, carry):
             acc = total[...]
-            for u in range(UNROLL):
-                k = step * UNROLL + u
-                prod = None
-                for t in range(2):
-                    image = jnp.dot(lhs[t], cheb[k, t], preferred_element_type=jnp.float32)
-                    term = image * fj[t]
-                    prod = term if prod is None else prod + term
-                if with_spare:
-                    image = jnp.dot(lhs_x[...], cheb_x[k], preferred_element_type=jnp.float32)
-                    prod = prod + image * fj[h]
-                narrow = prod[:, :LANES] + prod[:, LANES:]
-                moment = jnp.sum(narrow, axis=-1, keepdims=True)
-                acc = acc + moment * matrix[pl.ds(k, 1), :]
+            for u in range(SPARE_UNROLL):
+                k = step * SPARE_UNROLL + u
+                image = jnp.dot(lhs_x[...], cheb_x[k], preferred_element_type=jnp.float32)
+                acc = add_moment(acc, image * fj[h], base + k)
             total[...] = acc
             return carry
 
-        lax.fori_loop(0, LEVELS // UNROLL, body, 0)
-
-    @pl.when(off)
-    def _():
-        levels(False)
-
-    @pl.when(diagonal)
-    def _():
-        levels(True)
+        lax.fori_loop(0, HALF // SPARE_UNROLL, spare_step, 0)
 
     share[...] = total[...].T[:L]
 
@@ -367,7 +426,7 @@
         spread_line(e, lax.rem(r - e + n_rows, n_rows)).wait_recv()
 
     for s in range(len(order)):
-        scatter(s).wait_send()
+        copy(parcel.at[0], landed.at[s], send1.at[s], recv1.at[s], (r, peer(order[s]))).wait_send()
         gather(s).wait_send()
         exchange(s).wait_send()
     for e in LINE:
@@ -377,10 +436,23 @@
 
     @pl.when(diagonal)
     def _():
+        spare_cos().wait_send()
+        spare_rows().wait_send()
         for j in range(half_n):
             @pl.when(me != h * half_n + j)
             def _():
-                scatter_rest(j).wait_send()
+                copy(rest.at[j], landed_rest, send_rest.at[j], recv_rest.at[0], (r, c)).wait_send()
+
+
+def close_kernel(filtered, spectra, filtered_out, spectra_out, sem):
+    copies = [
+        pltpu.make_async_copy(filtered, filtered_out, sem.at[0]),
+        pltpu.make_async_copy(spectra, spectra_out, sem.at[1]),
+    ]
+    for copy in copies:
+        copy.start()
+    for copy in copies:
+        copy.wait()
 
 
 def per_device(npix, n_rows, n_cols, inverse_cov, cosines, sky_maps):
@@ -413,7 +485,7 @@
             pltpu.VMEM((5 * TILE, TILE), f32),
             pltpu.VMEM(matrix.shape, f32),
             pltpu.VMEM((LEVELS, 2, 2 * TILE, TILE), bf16),
-            pltpu.VMEM((LEVELS, TILE, TILE), bf16),
+            pltpu.VMEM((HALF, TILE, TILE), bf16),
             pltpu.VMEM((n, per, width), f32),
             pltpu.VMEM((n, per, width), bf16),
             pltpu.VMEM((n - 1, per, width), bf16),
@@ -423,6 +495,7 @@
             pltpu.VMEM((maps, cols_here), bf16),
             pltpu.VMEM((2, maps, 2 * TILE), bf16),
             pltpu.VMEM((maps, TILE), bf16),
+            pltpu.VMEM((maps, TILE), bf16),
             pltpu.VMEM((2, maps, TILE), f32),
             pltpu.VMEM((maps, LANES), f32),
             pltpu.VMEM((L, maps), f32),
@@ -431,14 +504,25 @@
             pltpu.VMEM((n, piece, maps), f32),
             pltpu.VMEM((piece, maps), f32),
             pltpu.SemaphoreType.DMA((8,)),
-            plane, plane, half, pltpu.SemaphoreType.DMA, plane, pltpu.SemaphoreType.DMA((n,)),
+            plane, pltpu.SemaphoreType.DMA((PARTS * (n - 1),)), half, pltpu.SemaphoreType.DMA((PARTS,)),
+            plane, pltpu.SemaphoreType.DMA((n,)),
             line, half, line, line, plane, plane, line, line,
+            pltpu.SemaphoreType.DMA((2,)), pltpu.SemaphoreType.DMA((2,)),
         ],
         compiler_params=pltpu.CompilerParams(
             collective_id=1, has_side_effects=True, vmem_limit_bytes=50 * 2**20
         ),
         name="qml",
     )(*[pltpu.with_memory_space_constraint(value, pltpu.HBM) for value in inputs])
+    filtered, spectra = pl.pallas_call(
+        close_kernel,
+        out_shape=(pltpu.HBM(filtered.shape, bf16), pltpu.HBM(spectra.shape, f32)),
+        in_specs=[vmem, vmem],
+        out_specs=(hbm, hbm),
+        scratch_shapes=[pltpu.SemaphoreType.DMA((2,))],
+        compiler_params=pltpu.CompilerParams(vmem_limit_bytes=2**20),
+        name="close",
+    )(filtered, spectra)
     return filtered.T, spectra
 
 

time: 49.4 us -> 46.3 us (0.937)
  Pallas kernels: 47.2 us -> 45.5 us
  local copies, waits for them, and re-layouts: 1.38 us -> 0 us
    pallas_call x1, Pallas kernels: 47.2 us -> 44.7 us  [per_device(): pl.pallas_call(functools.partial(qml_kernel, n_rows, n_z, N_X), out_shape...]
    unnamed x2 -> x0, local copies, waits for them, and re-layouts: 1.38 us -> none
    pallas_call x0 -> x1, Pallas kernels: none -> 0.78 us  [per_device(): pl.pallas_call(close_kernel, out_shape=(pltpu.HBM(filtered.shape, bf16),...]
where the time goes in v5:
time: 46.3 us; the launch traced here: 46.2 us
  Pallas kernels  45.5 us (98%)
  between operations  0.64 us (1%)
    pallas_call x1, Pallas kernels, per_device(): pl.pallas_call(functools.partial(qml_kernel, n_rows, n_z, N_X), out_shape...  44.7 us

profile of v5, /device:TPU:1, one launch (start us, length us, event | category | flops | bytes accessed | tf_op | source)
XLA Modules:
  0.0 46.2 jit_solution(10710437539944776408)
XLA Ops:
  0.6 44.7 %qml.1 = (bf16[192,1024]{1,0:T(8,128)(2,1)S(1)}, f32[64,192]{1,0:T(8,128)S(1)}) custom-call(bf16[192,512]{1,0:T(8,128)(2,1)} %bitcast.2, bf16[1024,512]{1,0:T(8,128)(2,1)} %cov_hbm.1, f32[1024,512]{1,0:T(8,128)} %cos_hbm.1, f32[72,128]{1,0:T(8,128)} %constant.2.clone.matrix_hbm), custom_call_target="tpu_custom_call" | custom-call | tf_op jit(solution)/shard_map/qml/pallas_call | solution.py:474
  45.4 0.8 %close.1 = (bf16[192,1024]{1,0:T(8,128)(2,1)}, f32[64,192]{1,0:T(8,128)}) custom-call(bf16[192,1024]{1,0:T(8,128)(2,1)S(1)} %get-tuple-element.6.filtered, f32[64,192]{1,0:T(8,128)S(1)} %get-tuple-element.7.spectra), custom_call_target="tpu_custom_call" | custom-call | tf_op jit(solution)/shard_map/close/pallas_call | solution.py:517

commit v6 on v5

--- a/solution.py
+++ b/solution.py
@@ -64,6 +64,7 @@
     off = r != q
     partner = r + 1 - 2 * lax.rem(r, 2)
     helper = partner == q
+    lead = lax.rem(r, 2) == 1
     side = jnp.where(r > q, h, 1 - h)
     barrier = pltpu.get_barrier_semaphore()
 
@@ -225,6 +226,15 @@
 
     generate_pair(0)
 
+    @pl.when(diagonal)
+    def _():
+        def store(k, at, value):
+            if k >= HALF:
+                cheb_x[k - HALF, pl.ds(at, STRIP), :] = value
+
+        lax.fori_loop(0, TILE // STRIP, generate(4 * TILE, store), 0)
+
+
     chunk_half = me // half_n
     has_rest = c != 2 * r + chunk_half
 
@@ -283,14 +293,6 @@
 
     generate_pair(1)
 
-    @pl.when(diagonal)
-    def _():
-        def store(k, at, value):
-            if k >= HALF:
-                cheb_x[k - HALF, pl.ds(at, STRIP), :] = value
-
-        lax.fori_loop(0, TILE // STRIP, generate(4 * TILE, store), 0)
-
     @pl.when(helper)
     def _():
         def store(k, at, value):
@@ -378,61 +380,95 @@
 
     share[...] = total[...].T[:L]
 
-    piece = L // n_rows
+    chips = n_rows // 2
+    piece = L // chips
+    core, y = lax.rem(r, 2), r // 2
 
     def block(k):
         return pl.ds(pl.multiple_of(k * piece, piece), piece)
 
-    def reduce_line(e):
+    def across(d):
+        return lax.rem(y + d, chips)
+
+    def reduce_line(d, source=core):
+        k = across(d)
         return copy(
-            share.at[block(line(e))], line_landed.at[e - 1], send4.at[e - 1], recv4.at[e - 1], (line(e), c)
+            share.at[block(k)], line_landed.at[2 * d + source], send4.at[d], recv4.at[2 * d + source],
+            (2 * k + 1, c),
         )
 
     def exchange(s):
         return copy(line_sum, plane_landed.at[c], send5.at[s], recv5.at[s], (r, peer(order[s])))
 
-    def spread_line(e, k):
-        return copy(result, spectra_out.at[block(k)], send6.at[e - 1], recv6.at[e - 1], (line(e), c))
-
-    for e in LINE:
-        reduce_line(e).start()
-
-    for k in range(n):
-        needed = jnp.logical_or(diagonal, side == k // half_n)
-
-        @pl.when(jnp.logical_and(jnp.logical_not(needed), me != k))
-        def _():
-            gathered(k).wait_recv()
-
-    for e in LINE:
-        reduce_line(e).wait_recv()
-    value = share[block(r)]
-    for e in range(1, n_rows):
-        value = value + line_landed[e - 1]
-    line_sum[...] = value
-    for s in range(len(order)):
-        exchange(s).start()
-    plane_landed[c] = value
-    for s in range(len(order)):
-        exchange(s).wait_recv()
-    value = plane_landed[0]
-    for k in range(1, n):
-        value = value + plane_landed[k]
-    result[...] = value
-    for e in LINE:
-        spread_line(e, r).start()
-    spectra_out[block(r)] = value
-    for e in LINE:
-        spread_line(e, lax.rem(r - e + n_rows, n_rows)).wait_recv()
+    def spread_line(d, target, k):
+        return copy(
+            result, spectra_out.at[block(k)], send6.at[2 * d + target], recv6.at[d], (2 * across(d) + target, c)
+        )
+
+    def finish_rows():
+        for k in range(n):
+            needed = jnp.logical_or(diagonal, side == k // half_n)
+
+            @pl.when(jnp.logical_and(jnp.logical_not(needed), me != k))
+            def _():
+                gathered(k).wait_recv()
+
+    for d in (2, 3, 1):
+        reduce_line(d).start()
+
+    @pl.when(jnp.logical_not(lead))
+    def _():
+        reduce_line(0, 0).start()
+
+    finish_rows()
+
+    @pl.when(lead)
+    def _():
+        value = share[block(y)]
+        for d, source in ((0, 0), (1, 0), (1, 1), (3, 0), (3, 1), (2, 0), (2, 1)):
+            reduce_line(d, source).wait_recv()
+            value = value + line_landed[2 * d + source]
+        line_sum[...] = value
+        for s in range(len(order)):
+            exchange(s).start()
+        plane_landed[c] = value
+        for s in range(len(order)):
+            exchange(s).wait_recv()
+        value = plane_landed[0]
+        for k in range(1, n):
+            value = value + plane_landed[k]
+        result[...] = value
+        for d in (2, 3, 1):
+            for target in range(2):
+                spread_line(d, target, y).start()
+        spread_line(0, 0, y).start()
+        spectra_out[block(y)] = value
+
+    for d in (1, 3, 2):
+        spread_line(d, 0, lax.rem(y - d + chips, chips)).wait_recv()
+
+    @pl.when(jnp.logical_not(lead))
+    def _():
+        spread_line(0, 0, y).wait_recv()
+        reduce_line(0, 0).wait_send()
+
+    for d in (1, 2, 3):
+        reduce_line(d).wait_send()
+
+    @pl.when(lead)
+    def _():
+        for s in range(len(order)):
+            exchange(s).wait_send()
+        for d in (1, 2, 3):
+            for target in range(2):
+                spread_line(d, target, y).wait_send()
+        spread_line(0, 0, y).wait_send()
 
     for s in range(len(order)):
         copy(parcel.at[0], landed.at[s], send1.at[s], recv1.at[s], (r, peer(order[s]))).wait_send()
         gather(s).wait_send()
-        exchange(s).wait_send()
     for e in LINE:
         column(e).wait_send()
-        reduce_line(e).wait_send()
-        spread_line(e, r).wait_send()
 
     @pl.when(diagonal)
     def _():
@@ -462,7 +498,7 @@
     maps = sky_maps.shape[1]
     sky_t = sky_maps.T
     per, width = maps // 2, 2 * size // n
-    piece = L // n_rows
+    piece = L // (n_rows // 2)
     vmem = pl.BlockSpec(memory_space=pltpu.VMEM)
     hbm = pl.BlockSpec(memory_space=pltpu.HBM)
     matrix = jnp.asarray(transform_matrix(npix))
@@ -471,6 +507,7 @@
     plane = pltpu.SemaphoreType.DMA((n - 1,))
     line = pltpu.SemaphoreType.DMA((n_rows - 1,))
     half = pltpu.SemaphoreType.DMA((n // 2,))
+    every = pltpu.SemaphoreType.DMA((n_rows,))
     filtered, spectra = pl.pallas_call(
         functools.partial(qml_kernel, n_rows, n_z, N_X),
         out_shape=(
@@ -499,14 +536,14 @@
             pltpu.VMEM((2, maps, TILE), f32),
             pltpu.VMEM((maps, LANES), f32),
             pltpu.VMEM((L, maps), f32),
-            pltpu.VMEM((n_rows - 1, piece, maps), f32),
+            pltpu.VMEM((n_rows, piece, maps), f32),
             pltpu.VMEM((piece, maps), f32),
             pltpu.VMEM((n, piece, maps), f32),
             pltpu.VMEM((piece, maps), f32),
             pltpu.SemaphoreType.DMA((8,)),
             plane, pltpu.SemaphoreType.DMA((PARTS * (n - 1),)), half, pltpu.SemaphoreType.DMA((PARTS,)),
             plane, pltpu.SemaphoreType.DMA((n,)),
-            line, half, line, line, plane, plane, line, line,
+            line, half, line, every, plane, plane, every, line,
             pltpu.SemaphoreType.DMA((2,)), pltpu.SemaphoreType.DMA((2,)),
         ],
         compiler_params=pltpu.CompilerParams(

time: 46.3 us -> 45.1 us (0.974)
  Pallas kernels: 45.5 us -> 44.3 us
    pallas_call x1, Pallas kernels: 44.7 us -> 43.6 us  [per_device(): pl.pallas_call(functools.partial(qml_kernel, n_rows, n_z, N_X), out_shape...]
where the time goes in v6:
time: 45.1 us; the launch traced here: 45 us
  Pallas kernels  44.3 us (98%)
  between operations  0.64 us (1%)
    pallas_call x1, Pallas kernels, per_device(): pl.pallas_call(functools.partial(qml_kernel, n_rows, n_z, N_X), out_shape...  43.6 us

profile of v6, /device:TPU:1, one launch (start us, length us, event | category | flops | bytes accessed | tf_op | source)
XLA Modules:
  0.0 45.0 jit_solution(14908723869662328437)
XLA Ops:
  0.6 43.6 %qml.1 = (bf16[192,1024]{1,0:T(8,128)(2,1)S(1)}, f32[64,192]{1,0:T(8,128)S(1)}) custom-call(bf16[192,512]{1,0:T(8,128)(2,1)} %bitcast.2, bf16[1024,512]{1,0:T(8,128)(2,1)} %cov_hbm.1, f32[1024,512]{1,0:T(8,128)} %cos_hbm.1, f32[72,128]{1,0:T(8,128)} %constant.2.clone.matrix_hbm), custom_call_target="tpu_custom_call" | custom-call | tf_op jit(solution)/shard_map/qml/pallas_call | solution.py:511
  44.2 0.8 %close.1 = (bf16[192,1024]{1,0:T(8,128)(2,1)}, f32[64,192]{1,0:T(8,128)}) custom-call(bf16[192,1024]{1,0:T(8,128)(2,1)S(1)} %get-tuple-element.6.filtered, f32[64,192]{1,0:T(8,128)S(1)} %get-tuple-element.7.spectra), custom_call_target="tpu_custom_call" | custom-call | tf_op jit(solution)/shard_map/close/pallas_call | solution.py:554

commit v7 on v6

--- a/solution.py
+++ b/solution.py
@@ -40,6 +40,7 @@
 
 
 LINE = [4, 5, 3, 2, 6, 1, 7]
+SAME = [4, 2, 6]
 
 
 def qml_kernel(
@@ -49,7 +50,7 @@
     sky, cov, cos, matrix, cheb, cheb_x, part, parcel, landed, rest, landed_rest, mine, cols,
     lhs, lhs_x, rows_x, fj, total, share, line_landed, line_sum, plane_landed, result,
     load_sem, send1, recv1, send_rest, recv_rest, send2, recv2, send3, recv3,
-    send4, recv4, send5, recv5, send6, recv6, send_x, recv_x,
+    send4, recv4, send5, recv5, send6, recv6, send_x, recv_x, send_r,
 ):
     r = lax.axis_index("prow")
     c = lax.axis_index("pcol")
@@ -64,6 +65,8 @@
     off = r != q
     partner = r + 1 - 2 * lax.rem(r, 2)
     helper = partner == q
+    relays = lax.rem(r + q, 2) == 0
+    relayed = lax.rem(r + q, 2) == 1
     lead = lax.rem(r, 2) == 1
     side = jnp.where(r > q, h, 1 - h)
     barrier = pltpu.get_barrier_semaphore()
@@ -126,7 +129,7 @@
     for e in LINE:
         signal((line(e), c))
 
-    @pl.when(off)
+    @pl.when(jnp.logical_and(off, relays))
     def _():
         for j in range(half_n):
             signal((q, owner(q, h * half_n + j)))
@@ -154,7 +157,7 @@
                 part[k] = piece
                 parcel[k] = piece.astype(jnp.bfloat16)
 
-    pl.semaphore_wait(barrier, len(order) + 2 * (n_rows - 1))
+    pl.semaphore_wait(barrier, len(order) + len(LINE) + len(SAME))
 
     def part_of(ref, p):
         return ref.at[pl.ds(p * (per // PARTS), per // PARTS)]
@@ -252,7 +255,7 @@
 
     def column(e, cut=lambda ref: ref):
         return copy(
-            cut(mine), cut(place(cols, lax.rem(me, half_n))), send3.at[e - 1], recv3.at[lax.rem(me, half_n)],
+            cut(mine), cut(place(cols, lax.rem(me, half_n))), send3.at[e // 2 - 1], recv3.at[lax.rem(me, half_n)],
             (line(e), 2 * r + chunk_half),
         )
 
@@ -278,14 +281,12 @@
             part[me, span] = part[me, span] + landed_rest[span].astype(jnp.float32)
 
         mine[span] = part[me, span].astype(jnp.bfloat16)
-        for e in LINE[:4]:
+        for e in SAME:
             column(e, cut).start()
         for s in range(len(order)):
             @pl.when(wanted(peer(order[s])))
             def _():
                 gather(s, cut).start()
-        for e in LINE[4:]:
-            column(e, cut).start()
     rows[
         pl.ds(pl.multiple_of(lax.rem(me, 2) * per, per), per),
         pl.ds(pl.multiple_of((me // 2) * width, width), width),
@@ -301,30 +302,51 @@
         spare_cos().wait_recv()
         lax.fori_loop(0, TILE // STRIP, generate(4 * TILE, store, HALF), 0)
 
+    def relay(j, source):
+        return copy(source, place(cols, j), send_r.at[j], recv3.at[j], (partner, c))
+
+    def arrived(j):
+        return copy(mine, place(cols, j), send3.at[0], recv3.at[j], (q, owner(q, h * half_n + j)))
+
+    @pl.when(jnp.logical_and(off, relays))
+    def _():
+        for j in range(half_n):
+            arrived(j).wait_recv()
+            relay(j, place(cols, j)).start()
+
+    @pl.when(diagonal)
+    def _():
+        for j in range(half_n):
+            k = h * half_n + j
+
+            @pl.when(me != k)
+            def _():
+                gathered(k).wait_recv()
+
+            relay(j, place(rows, k)).start()
+
+    for k in range(n):
+        needed = jnp.where(diagonal, h != k // half_n, side == k // half_n)
+
+        @pl.when(jnp.logical_and(needed, me != k))
+        def _():
+            gathered(k).wait_recv()
+
+    @pl.when(relayed)
+    def _():
+        for j in range(half_n):
+            arrived(j).wait_recv()
+
+    @pl.when(diagonal)
+    def _():
+        spare_rows().start()
+        size = cols.shape[1]
+        cols[...] = rows[:, pl.ds(pl.multiple_of(h * size, size), size)]
+
     for s in range(len(order)):
         @pl.when(jnp.logical_not(wanted(peer(order[s]))))
         def _():
             gather(s).start()
-
-    for k in range(n):
-        needed = jnp.logical_or(diagonal, side == k // half_n)
-
-        @pl.when(jnp.logical_and(needed, me != k))
-        def _():
-            gathered(k).wait_recv()
-
-    @pl.when(off)
-    def _():
-        for j in range(half_n):
-            copy(
-                mine, place(cols, j), send3.at[0], recv3.at[j], (q, owner(q, h * half_n + j))
-            ).wait_recv()
-
-    @pl.when(diagonal)
-    def _():
-        spare_rows().start()
-        size = cols.shape[1]
-        cols[...] = rows[:, pl.ds(pl.multiple_of(h * size, size), size)]
 
     weight = jnp.where(diagonal, 1, 2).astype(jnp.float32)
     for t in range(2):
@@ -464,10 +486,15 @@
                 spread_line(d, target, y).wait_send()
         spread_line(0, 0, y).wait_send()
 
+    @pl.when(relays)
+    def _():
+        for j in range(half_n):
+            relay(j, place(cols, j)).wait_send()
+
     for s in range(len(order)):
         copy(parcel.at[0], landed.at[s], send1.at[s], recv1.at[s], (r, peer(order[s]))).wait_send()
         gather(s).wait_send()
-    for e in LINE:
+    for e in SAME:
         column(e).wait_send()
 
     @pl.when(diagonal)
@@ -544,7 +571,7 @@
             plane, pltpu.SemaphoreType.DMA((PARTS * (n - 1),)), half, pltpu.SemaphoreType.DMA((PARTS,)),
             plane, pltpu.SemaphoreType.DMA((n,)),
             line, half, line, every, plane, plane, every, line,
-            pltpu.SemaphoreType.DMA((2,)), pltpu.SemaphoreType.DMA((2,)),
+            pltpu.SemaphoreType.DMA((2,)), pltpu.SemaphoreType.DMA((2,)), half,
         ],
         compiler_params=pltpu.CompilerParams(
             collective_id=1, has_side_effects=True, vmem_limit_bytes=50 * 2**20

time: 45.1 us -> 44.7 us (level)
    pallas_call x1, Pallas kernels: 43.6 us -> 43.1 us  [per_device(): pl.pallas_call(functools.partial(qml_kernel, n_rows, n_z, N_X), out_shape...]
where the time goes in v7:
time: 44.7 us; the launch traced here: 44.5 us
  Pallas kernels  43.9 us (98%)
  between operations  0.64 us (1%)
    pallas_call x1, Pallas kernels, per_device(): pl.pallas_call(functools.partial(qml_kernel, n_rows, n_z, N_X), out_shape...  43.1 us

profile of v7, /device:TPU:1, one launch (start us, length us, event | category | flops | bytes accessed | tf_op | source)
XLA Modules:
  0.0 44.5 jit_solution(7330270053468321474)
XLA Ops:
  0.6 43.1 %qml.1 = (bf16[192,1024]{1,0:T(8,128)(2,1)S(1)}, f32[64,192]{1,0:T(8,128)S(1)}) custom-call(bf16[192,512]{1,0:T(8,128)(2,1)} %bitcast.2, bf16[1024,512]{1,0:T(8,128)(2,1)} %cov_hbm.1, f32[1024,512]{1,0:T(8,128)} %cos_hbm.1, f32[72,128]{1,0:T(8,128)} %constant.2.clone.matrix_hbm), custom_call_target="tpu_custom_call" | custom-call | tf_op jit(solution)/shard_map/qml/pallas_call | solution.py:538
  43.7 0.8 %close.1 = (bf16[192,1024]{1,0:T(8,128)(2,1)}, f32[64,192]{1,0:T(8,128)}) custom-call(bf16[192,1024]{1,0:T(8,128)(2,1)S(1)} %get-tuple-element.6.filtered, f32[64,192]{1,0:T(8,128)S(1)} %get-tuple-element.7.spectra), custom_call_target="tpu_custom_call" | custom-call | tf_op jit(solution)/shard_map/close/pallas_call | solution.py:581

commit v8 on v7

--- a/solution.py
+++ b/solution.py
@@ -65,9 +65,9 @@
     off = r != q
     partner = r + 1 - 2 * lax.rem(r, 2)
     helper = partner == q
-    relays = lax.rem(r + q, 2) == 0
-    relayed = lax.rem(r + q, 2) == 1
     lead = lax.rem(r, 2) == 1
+    relays = jnp.logical_or(diagonal, jnp.logical_and(r // 2 != q // 2, lead))
+    relayed = jnp.logical_not(relays)
     side = jnp.where(r > q, h, 1 - h)
     barrier = pltpu.get_barrier_semaphore()
 
@@ -256,7 +256,7 @@
     def column(e, cut=lambda ref: ref):
         return copy(
             cut(mine), cut(place(cols, lax.rem(me, half_n))), send3.at[e // 2 - 1], recv3.at[lax.rem(me, half_n)],
-            (line(e), 2 * r + chunk_half),
+            (line(e) // 2 * 2 + 1, 2 * r + chunk_half),
         )
 
     def wanted(to):
@@ -313,6 +313,8 @@
         for j in range(half_n):
             arrived(j).wait_recv()
             relay(j, place(cols, j)).start()
+        for t in range(2):
+            fj[t] = cols[:, t * TILE : (t + 1) * TILE].astype(jnp.float32)
 
     @pl.when(diagonal)
     def _():
@@ -324,6 +326,8 @@
                 gathered(k).wait_recv()
 
             relay(j, place(rows, k)).start()
+        for t in range(2):
+            fj[t] = rows[:, tile_at(2 * h + t)].astype(jnp.float32)
 
     for k in range(n):
         needed = jnp.where(diagonal, h != k // half_n, side == k // half_n)
@@ -332,16 +336,9 @@
         def _():
             gathered(k).wait_recv()
 
-    @pl.when(relayed)
-    def _():
-        for j in range(half_n):
-            arrived(j).wait_recv()
-
     @pl.when(diagonal)
     def _():
         spare_rows().start()
-        size = cols.shape[1]
-        cols[...] = rows[:, pl.ds(pl.multiple_of(h * size, size), size)]
 
     for s in range(len(order)):
         @pl.when(jnp.logical_not(wanted(peer(order[s]))))
@@ -352,7 +349,13 @@
     for t in range(2):
         lhs[t, :, :TILE] = (rows[:, tile_at(first[t])].astype(jnp.float32) * weight).astype(jnp.bfloat16)
         lhs[t, :, TILE:] = (rows[:, tile_at(second[t])].astype(jnp.float32) * 2.0).astype(jnp.bfloat16)
-        fj[t] = cols[:, t * TILE : (t + 1) * TILE].astype(jnp.float32)
+
+    @pl.when(relayed)
+    def _():
+        for j in range(half_n):
+            arrived(j).wait_recv()
+        for t in range(2):
+            fj[t] = cols[:, t * TILE : (t + 1) * TILE].astype(jnp.float32)
 
     matrix_load.wait()
     total[...] = jnp.zeros_like(total)

time: 44.7 us -> 44.4 us (level)
  no operation moved by 1% of the time
where the time goes in v8:
time: 44.4 us; the launch traced here: 44.3 us
  Pallas kernels  43.6 us (98%)
  between operations  0.64 us (1%)
    pallas_call x1, Pallas kernels, per_device(): pl.pallas_call(functools.partial(qml_kernel, n_rows, n_z, N_X), out_shape...  42.9 us

profile of v8, /device:TPU:1, one launch (start us, length us, event | category | flops | bytes accessed | tf_op | source)
XLA Modules:
  0.0 44.3 jit_solution(16973525947533117051)
XLA Ops:
  0.6 42.9 %qml.1 = (bf16[192,1024]{1,0:T(8,128)(2,1)S(1)}, f32[64,192]{1,0:T(8,128)S(1)}) custom-call(bf16[192,512]{1,0:T(8,128)(2,1)} %bitcast.2, bf16[1024,512]{1,0:T(8,128)(2,1)} %cov_hbm.1, f32[1024,512]{1,0:T(8,128)} %cos_hbm.1, f32[72,128]{1,0:T(8,128)} %constant.2.clone.matrix_hbm), custom_call_target="tpu_custom_call" | custom-call | tf_op jit(solution)/shard_map/qml/pallas_call | solution.py:541
  43.5 0.8 %close.1 = (bf16[192,1024]{1,0:T(8,128)(2,1)}, f32[64,192]{1,0:T(8,128)}) custom-call(bf16[192,1024]{1,0:T(8,128)(2,1)S(1)} %get-tuple-element.6.filtered, f32[64,192]{1,0:T(8,128)S(1)} %get-tuple-element.7.spectra), custom_call_target="tpu_custom_call" | custom-call | tf_op jit(solution)/shard_map/close/pallas_call | solution.py:584

commit v9 on v8

--- a/solution.py
+++ b/solution.py
@@ -34,9 +34,12 @@
 
 
 def rank_order(rows, cols):
-    spots = [(dz, dx) for dz in range(rows) for dx in range(cols) if dz or dx]
-    reach = lambda d, n: min(d, n - d)
-    return sorted(spots, key=lambda s: -(reach(s[0], rows) + reach(s[1], cols)))
+    spots = [
+        (2, 2), (1, 1), (3, 3), (1, 3), (3, 1), (2, 1), (1, 2), (2, 3), (3, 2),
+        (0, 1), (1, 0), (0, 3), (3, 0), (0, 2), (2, 0),
+    ]
+    assert (rows, cols) == (4, 4)
+    return spots
 
 
 LINE = [4, 5, 3, 2, 6, 1, 7]

time: 44.4 us -> 44.4 us (level)
  no operation moved by 1% of the time
where the time goes in v9:
time: 44.4 us; the launch traced here: 44.3 us
  Pallas kernels  43.7 us (98%)
  between operations  0.64 us (1%)
    pallas_call x1, Pallas kernels, per_device(): pl.pallas_call(functools.partial(qml_kernel, n_rows, n_z, N_X), out_shape...  42.9 us

profile of v9, /device:TPU:1, one launch (start us, length us, event | category | flops | bytes accessed | tf_op | source)
XLA Modules:
  0.0 44.3 jit_solution(900808687173922653)
XLA Ops:
  0.6 42.9 %qml.1 = (bf16[192,1024]{1,0:T(8,128)(2,1)S(1)}, f32[64,192]{1,0:T(8,128)S(1)}) custom-call(bf16[192,512]{1,0:T(8,128)(2,1)} %bitcast.2, bf16[1024,512]{1,0:T(8,128)(2,1)} %cov_hbm.1, f32[1024,512]{1,0:T(8,128)} %cos_hbm.1, f32[72,128]{1,0:T(8,128)} %constant.2.clone.matrix_hbm), custom_call_target="tpu_custom_call" | custom-call | tf_op jit(solution)/shard_map/qml/pallas_call | solution.py:544
  43.5 0.8 %close.1 = (bf16[192,1024]{1,0:T(8,128)(2,1)}, f32[64,192]{1,0:T(8,128)}) custom-call(bf16[192,1024]{1,0:T(8,128)(2,1)S(1)} %get-tuple-element.6.filtered, f32[64,192]{1,0:T(8,128)S(1)} %get-tuple-element.7.spectra), custom_call_target="tpu_custom_call" | custom-call | tf_op jit(solution)/shard_map/close/pallas_call | solution.py:587
